TPU v7x, 512 devices: a whole 4x8x8 slice. The times are simulated.
512 devices in a mesh: gx: 16 (over y, core), gy: 32 (over x, z).
Axes of the slice: x: 4, y: 8, z: 8, core: 2. Of those that a mesh axis runs over, the one named last changes fastest.
Arguments:
- incident: float32 [64, 512, 240], P('gx', 'gy'), may hold values from -13 to 13
- sphere_kinds: int32 [64, 512], P('gx', 'gy'), may hold values from 0 to 3
- pair_codes: int32 [64, 512, 64], P('gx', 'gy'), may hold values from 0 to 80
- operators: int32 [64, 512, 64], P('gx', 'gy'), may hold values from 0 to 23
- pair_valid: int32 [64, 512, 64], P('gx', 'gy'), may hold values 0 or 1
- translations: bfloat16 [24, 240, 240], replicated, may hold values from -0.03125 to 0.03125
- tmatrices: float32 [4, 240, 240], replicated, may hold values from -0.375 to 0.375
Outputs:
- solution: float32 [64, 512, 240], P('gx', 'gy')
- residual: float32 [64, 512, 240], P('gx', 'gy')
All inputs are finite; a program needn't handle non-finite values. No bound on the sum of `pair_valid` on one device may be relied on, other than what follows from the above.
Results may differ from a plain program's by a relative error of at most 0.0038.
Values sent between devices are 32-bit elements; how exact they have to be, the bound alone decides.
A program may use at most 64 MiB of HBM per device.

v0:
```python
import jax
import jax.numpy as jnp
from jax import lax
from jax.sharding import Mesh
from jax.sharding import PartitionSpec as P

HALO = 4
GX = ("gx_0", "gx_1")
GY = ("gy_0", "gy_1")


epsilon = 1e-06


def with_halo(cells, sides, width):
    for axis, dim in sides:
        count = lax.axis_size(axis)
        ends = count - 1
        head = lax.slice_in_dim(cells, 0, width, axis=dim)
        tail = lax.slice_in_dim(cells, cells.shape[dim] - width, cells.shape[dim], axis=dim)
        cells = jnp.concatenate(
            [
                lax.ppermute(tail, axis, [(i, (i + 1) % count) for i in range(ends)]),
                cells,
                lax.ppermute(head, axis, [((i + 1) % count, i) for i in range(ends)]),
            ],
            axis=dim,
        )
    return cells


def copy_for_each(shard, axis):
    devices = lax.axis_size(axis)
    return lax.all_to_all(
        jnp.broadcast_to(shard[None], (devices, *shard.shape)), axis, 0, 0, tiled=True
    )


def taken_together(shard, axis):
    return copy_for_each(shard, axis).sum(axis=0)


def over_axes(shard, axes):
    far, near = axes
    nearer = taken_together(shard, near)
    return taken_together(nearer, far)


def gather_plan(pair_codes, operators, pair_valid, count_ops, line_width):
    row_count, col_count, slot_count = pair_codes.shape
    stride = 2 * HALO + 1
    local_x = jnp.arange(row_count, dtype=jnp.int32)[:, None, None]
    local_y = jnp.arange(col_count, dtype=jnp.int32)[None, :, None]
    targets = (local_x + pair_codes // stride) * line_width + local_y + pair_codes % stride
    chosen = (operators[..., None] == jnp.arange(count_ops, dtype=jnp.int32)).astype(
        jnp.float32
    ) * pair_valid[..., None].astype(jnp.float32)
    return (
        targets.reshape(row_count * col_count, slot_count),
        chosen.reshape(row_count * col_count, slot_count, count_ops),
    )


def apply_kinds(tmatrices, selector, values):
    per_kind = jnp.einsum("pcd,id->pic", tmatrices, values, precision=lax.Precision.HIGHEST)
    return jnp.einsum("ip,pic->ic", selector, per_kind, precision=lax.Precision.HIGHEST)


def translate(values, targets, chosen, translations):
    extended = with_halo(values, ((GX, 0), (GY, 1)), HALO)
    flattened = extended.reshape(-1, extended.shape[2])
    picked = jnp.take(flattened, targets, axis=0)
    grouped = jnp.einsum("isk,isc->kic", chosen, picked, precision=lax.Precision.HIGHEST).astype(
        jnp.bfloat16
    )
    return jnp.einsum("kcd,kid->ic", translations, grouped, preferred_element_type=jnp.float32)


def merged_products(image, basis_list):
    partial_value = [jnp.sum(image * vector) for vector in basis_list] + [jnp.sum(image * image)]
    return over_axes(jnp.stack(partial_value), (("gx_0", "gx_1"), ("gy_0", "gy_1")))


def body(incident, sphere_kinds, pair_codes, operators, pair_valid, translations, tmatrices):
    row_count, col_count, coeffs = incident.shape
    targets, chosen = gather_plan(
        pair_codes, operators, pair_valid, translations.shape[0], col_count + 2 * HALO
    )
    selector = (
        sphere_kinds.reshape(-1)[:, None]
        == jnp.arange(tmatrices.shape[0], dtype=jnp.int32)[None, :]
    ).astype(jnp.float32)

    def apply_op(values):
        moved = translate(values, targets, chosen, translations)
        return values - apply_kinds(tmatrices, selector, moved).reshape(values.shape)

    source = apply_kinds(tmatrices, selector, incident.reshape(-1, coeffs)).reshape(incident.shape)
    beta = jnp.sqrt(
        over_axes(jnp.sum(source * source), (("gx_0", "gx_1"), ("gy_0", "gy_1"))) + epsilon
    )
    first = source / beta
    image_one = apply_op(first)
    totals = merged_products(image_one, [first])
    h_one_one = totals[0]
    h_two_one = jnp.sqrt(totals[1] - h_one_one * h_one_one + epsilon)
    second = (image_one - h_one_one * first) / h_two_one
    image_two = apply_op(second)
    totals = merged_products(image_two, [first, second])
    h_one_two = totals[0]
    h_two_two = totals[1]
    h_three_two = jnp.sqrt(totals[2] - h_one_two * h_one_two - h_two_two * h_two_two + epsilon)
    gram_aa = h_one_one * h_one_one + h_two_one * h_two_one
    gram_ab = h_one_one * h_one_two + h_two_one * h_two_two
    gram_bb = h_one_two * h_one_two + h_two_two * h_two_two + h_three_two * h_three_two
    right_a = beta * h_one_one
    right_b = beta * h_one_two
    determ = gram_aa * gram_bb - gram_ab * gram_ab
    coef_a = (gram_bb * right_a - gram_ab * right_b) / determ
    coef_b = (gram_aa * right_b - gram_ab * right_a) / determ
    solution = coef_a * first + coef_b * second
    residual = source - coef_a * image_one - coef_b * image_two
    return (solution, residual)


def solution(mesh):
    split = Mesh(mesh.devices.reshape(8, 2, 4, 8), ("gx_0", "gx_1", "gy_0", "gy_1"))
    in_specs = (
        P(GX, GY, None),
        P(GX, GY),
        P(GX, GY, None),
        P(GX, GY, None),
        P(GX, GY, None),
        P(),
        P(),
    )
    out_specs = (P(GX, GY, None), P(GX, GY, None))
    return jax.shard_map(body, mesh=split, in_specs=in_specs, out_specs=out_specs, check_vma=False)
```

profile of v0, /device:TPU:1, one launch (start us, length us, event | category | flops | bytes accessed | tf_op | source)
XLA Modules:
  0.0 201.9 jit_solution(39626812454283423)
XLA Ops:
  0.6 0.0 copy-start
  0.6 0.9 eq.33
  1.6 0.1 fusion.46
  1.6 2.3 %convolution_bitcast_fusion.2 = f32[4,64,240]{2,1,0:T(8,128)S(1)} fusion(f32[64,240,1]{1,0,2:T(8,128)} %bitcast.93, f32[4,240,240]{2,1,0:T(8,128)} %param.15), kind=kOutput, calls=%fused_computation.16 | convolution fusion | flops 176947200 | bytes 1228800 | tf_op jit(solution)/shard_map/pcd,id->pic/dot_general | solution.py:65
  3.9 0.5 fusion.36
  4.5 0.6 fusion.41
  5.1 1.3 broadcast_in_dim.21
  6.4 13.7 %all-to-all-start = ((f32[32,1,1]{2,1,0:T(1,128)}), f32[32,1,1]{2,1,0:T(1,128)S(1)}, u32[]{:S(2)}, u32[]{:S(2)}) async-start(f32[32,1,1]{2,1,0:T(1,128)} %broadcast_in_dim.21), calls=%async_computation | async-start | bytes 32768 | tf_op jit(solution)/shard_map/all_to_all | solution.py:34
  20.1 0.8 fusion.45
  20.9 7.8 %all-to-all-done = f32[32,1,1]{2,1,0:T(1,128)S(1)} async-done(((f32[32,1,1]{2,1,0:T(1,128)}), f32[32,1,1]{2,1,0:T(1,128)S(1)}, u32[]{:S(2)}, u32[]{:S(2)}) %all-to-all-start) | async-done | bytes 160 | tf_op jit(solution)/shard_map/all_to_all | solution.py:34
  28.7 0.6 reduce_sum.109
  29.3 1.2 broadcast_in_dim.22
  30.5 9.2 %all-to-all-start.1 = ((f32[16,1,1]{2,1,0:T(1,128)}), f32[16,1,1]{2,1,0:T(1,128)S(1)}, u32[]{:S(2)}, u32[]{:S(2)}) async-start(f32[16,1,1]{2,1,0:T(1,128)} %broadcast_in_dim.22), calls=%async_computation.1 | async-start | bytes 16384 | tf_op jit(solution)/shard_map/all_to_all | solution.py:34
  39.8 6.9 %all-to-all-done.1 = f32[16,1,1]{2,1,0:T(1,128)S(1)} async-done(((f32[16,1,1]{2,1,0:T(1,128)}), f32[16,1,1]{2,1,0:T(1,128)S(1)}, u32[]{:S(2)}, u32[]{:S(2)}) %all-to-all-start.1) | async-done | bytes 96 | tf_op jit(solution)/shard_map/all_to_all | solution.py:34
  46.7 0.6 reduce_sum.110
  48.1 2.7 %collective-permute-start = (f32[4,16,240]{2,1,0:T(8,128)S(1)}, f32[4,16,240]{2,1,0:T(8,128)S(1)}, u32[]{:S(2)}, u32[]{:S(2)}) collective-permute-start(f32[4,16,240]{2,1,0:T(8,128)S(1)} %broadcast_divide_fusion), channel_id=1, source_target_pairs={{0,32},{32,64},{64,96},{96,128},{128,160},{160,192},{192,224},{224... | collective-permute-start | bytes 184328 | tf_op jit(solution)/shard_map/ppermute | solution.py:23
  50.8 1.9 collective-permute-start.1
  52.7 0.6 compare_and_fusion
  53.3 0.1 reshape.96
  53.4 0.0 collective-permute-done
  53.4 3.0 %collective-permute-done.1 = f32[4,16,240]{2,1,0:T(8,128)S(1)} collective-permute-done((f32[4,16,240]{2,1,0:T(8,128)S(1)}, f32[4,16,240]{2,1,0:T(8,128)S(1)}, u32[]{:S(2)}, u32[]{:S(2)}) %collective-permute-start.1) | collective-permute-done | bytes 61472 | tf_op jit(solution)/shard_map/ppermute | solution.py:25
  56.4 2.2 %collective-permute-start.2 = (f32[12,4,240]{2,1,0:T(4,128)S(1)}, f32[12,4,240]{2,1,0:T(4,128)S(1)}, u32[]{:S(2)}, u32[]{:S(2)}) collective-permute-start(f32[12,4,240]{2,1,0:T(4,128)S(1)} %get-tuple-element.12), channel_id=1, source_target_pairs={{0,1},{1,2},{2,3},{3,4},{4,5},{5,6},{6,7},{7,8},{8,9},{9,10},{10,1... | collective-permute-start | bytes 138248 | tf_op jit(solution)/shard_map/ppermute | solution.py:23
  58.7 1.3 collective-permute-start.3
  60.0 0.8 convert_element_type.18
  60.7 2.7 %collective-permute-done.3 = f32[12,4,240]{2,1,0:T(4,128)S(1)} collective-permute-done((f32[12,4,240]{2,1,0:T(4,128)S(1)}, f32[12,4,240]{2,1,0:T(4,128)S(1)}, u32[]{:S(2)}, u32[]{:S(2)}) %collective-permute-start.3) | collective-permute-done | bytes 46112 | tf_op jit(solution)/shard_map/ppermute | solution.py:25
  63.5 0.9 pad_maximum_fusion
  64.4 0.0 copy-start.5
  64.4 0.0 copy-start.6
  64.4 16.1 %gather_fusion = f32[4096,240]{1,0:T(8,128)} fusion(f32[288,240]{1,0:T(8,128)S(1)} %bitcast.80, s32[4096]{0:T(1024)S(1)} %broadcast_clamp_fusion), kind=kCustom, calls=%fused_computation.clone | custom fusion | bytes 7880704 | tf_op jit(solution)/shard_map/jit(_take)/gather | solution.py:72
  80.5 4.6 %fusion.17 = bf16[24,64,240]{2,0,1:T(8,128)(2,1)S(1)} fusion(f32[64,64,240]{2,1,0:T(8,128)} %bitcast.83, pred[64,64]{1,0:T(8,128)(4,1)S(1)} %copy-done.6, f32[64,64]{1,0:T(8,128)S(1)} %bitcast.87, s32[64,64]{1,0:T(8,128)S(1)} %bitcast.92), kind=kOutput, calls=%fused_computation.13 | convolution fusion | flops 284663808 | bytes 4706304 | tf_op jit(solution)/shard_map/isk,isc->kic/dot_general | solution.py:73
  85.1 1.0 fusion.24
  86.2 1.0 convolution_bitcast_fusion.1
  87.2 0.5 fusion.34
  87.7 0.7 multiply_reduce_fusion.4
  88.5 1.4 pad_maximum_fusion.8
  89.9 16.1 %all_to_all.36 = f32[32,1,2]{2,1,0:T(1,128)S(1)} all-to-all(f32[32,1,2]{2,1,0:T(1,128)S(1)} %broadcast_in_dim.23), channel_id=1, replica_groups=mesh['gx_0'=8,'gx_1'=2,'gy_0'=4,'gy_1'=8] {'gy_0','gy_1'}, dimensions={0} | all-to-all | bytes 512 | tf_op jit(solution)/shard_map/all_to_all | solution.py:34
  106.0 0.1 reduce_sum.113
  106.0 0.6 broadcast_in_dim.24
  106.6 5.8 %all-to-all-start.3 = ((f32[16,1,2]{2,1,0:T(1,128)}), f32[16,1,2]{2,1,0:T(1,128)S(1)}, u32[]{:S(2)}, u32[]{:S(2)}) async-start(f32[16,1,2]{2,1,0:T(1,128)} %broadcast_in_dim.24), calls=%async_computation.3 | async-start | bytes 16384 | tf_op jit(solution)/shard_map/all_to_all | solution.py:34
  112.4 7.0 %all-to-all-done.3 = f32[16,1,2]{2,1,0:T(1,128)S(1)} async-done(((f32[16,1,2]{2,1,0:T(1,128)}), f32[16,1,2]{2,1,0:T(1,128)S(1)}, u32[]{:S(2)}, u32[]{:S(2)}) %all-to-all-start.3) | async-done | bytes 160 | tf_op jit(solution)/shard_map/all_to_all | solution.py:34
  119.4 0.6 fusion.53
  121.9 1.3 subtract_divide_fusion
  123.2 2.7 %collective-permute-start.4 = (f32[4,16,240]{2,1,0:T(8,128)S(1)}, f32[4,16,240]{2,1,0:T(8,128)S(1)}, u32[]{:S(2)}, u32[]{:S(2)}) collective-permute-start(f32[4,16,240]{2,1,0:T(8,128)S(1)} %get-tuple-element.8), channel_id=1, source_target_pairs={{0,32},{32,64},{64,96},{96,128},{128,160},{160,192},{192,224},{224... | collective-permute-start | bytes 184328 | tf_op jit(solution)/shard_map/ppermute | solution.py:23
  125.9 1.9 collective-permute-start.5
  127.8 3.6 %collective-permute-done.5 = f32[4,16,240]{2,1,0:T(8,128)S(1)} collective-permute-done((f32[4,16,240]{2,1,0:T(8,128)S(1)}, f32[4,16,240]{2,1,0:T(8,128)S(1)}, u32[]{:S(2)}, u32[]{:S(2)}) %collective-permute-start.5) | collective-permute-done | bytes 61472 | tf_op jit(solution)/shard_map/ppermute | solution.py:25
  131.5 2.2 %collective-permute-start.6 = (f32[12,4,240]{2,1,0:T(4,128)S(1)}, f32[12,4,240]{2,1,0:T(4,128)S(1)}, u32[]{:S(2)}, u32[]{:S(2)}) collective-permute-start(f32[12,4,240]{2,1,0:T(4,128)S(1)} %get-tuple-element.10), channel_id=1, source_target_pairs={{0,1},{1,2},{2,3},{3,4},{4,5},{5,6},{6,7},{7,8},{8,9},{9,10},{10,1... | collective-permute-start | bytes 138248 | tf_op jit(solution)/shard_map/ppermute | solution.py:23
  133.7 1.3 collective-permute-start.7
  135.0 3.5 %collective-permute-done.7 = f32[12,4,240]{2,1,0:T(4,128)S(1)} collective-permute-done((f32[12,4,240]{2,1,0:T(4,128)S(1)}, f32[12,4,240]{2,1,0:T(4,128)S(1)}, u32[]{:S(2)}, u32[]{:S(2)}) %collective-permute-start.7) | collective-permute-done | bytes 46112 | tf_op jit(solution)/shard_map/ppermute | solution.py:25
  138.6 0.1 pad_maximum_fusion.1
  138.6 16.1 %gather_fusion.1 = f32[4096,240]{1,0:T(8,128)} fusion(f32[288,240]{1,0:T(8,128)S(1)} %bitcast.81, s32[4096]{0:T(1024)S(1)} %broadcast_clamp_fusion), kind=kCustom, calls=%fused_computation.1.clone | custom fusion | bytes 7880704 | tf_op jit(solution)/shard_map/jit(_take)/gather | solution.py:72
  154.7 4.7 %fusion.14 = bf16[24,64,240]{2,0,1:T(8,128)(2,1)S(1)} fusion(f32[64,64,240]{2,1,0:T(8,128)} %bitcast.82, pred[64,64]{1,0:T(8,128)(4,1)} %compare_and_fusion, f32[64,64]{1,0:T(8,128)S(1)} %bitcast.88, s32[64,64]{1,0:T(8,128)} %bitcast.91), kind=kOutput, calls=%fused_computation.12 | convolution fusion | flops 284663808 | bytes 4706304 | tf_op jit(solution)/shard_map/isk,isc->kic/dot_general | solution.py:73
  159.4 0.0 copy-start.4
  159.4 1.0 fusion.22
  160.4 1.0 convolution_bitcast_fusion
  161.5 0.5 fusion.32
  162.0 1.3 multiply_reduce_fusion.2
  163.3 2.0 pad_maximum_fusion.9
  165.3 16.1 %all_to_all.37 = f32[32,1,3]{2,1,0:T(1,128)S(1)} all-to-all(f32[32,1,3]{2,1,0:T(1,128)S(1)} %broadcast_in_dim.25), channel_id=1, replica_groups=mesh['gx_0'=8,'gx_1'=2,'gy_0'=4,'gy_1'=8] {'gy_0','gy_1'}, dimensions={0} | all-to-all | bytes 768 | tf_op jit(solution)/shard_map/all_to_all | solution.py:34
  181.4 0.1 reduce_sum.118
  181.4 0.6 broadcast_in_dim.26
  182.0 5.8 %all-to-all-start.5 = ((f32[16,1,3]{2,1,0:T(1,128)}), f32[16,1,3]{2,1,0:T(1,128)S(1)}, u32[]{:S(2)}, u32[]{:S(2)}) async-start(f32[16,1,3]{2,1,0:T(1,128)} %broadcast_in_dim.26), calls=%async_computation.5 | async-start | bytes 16384 | tf_op jit(solution)/shard_map/all_to_all | solution.py:34
  188.4 6.3 %all-to-all-done.5 = f32[16,1,3]{2,1,0:T(1,128)S(1)} async-done(((f32[16,1,3]{2,1,0:T(1,128)}), f32[16,1,3]{2,1,0:T(1,128)S(1)}, u32[]{:S(2)}, u32[]{:S(2)}) %all-to-all-start.5) | async-done | bytes 224 | tf_op jit(solution)/shard_map/all_to_all | solution.py:34
  194.8 0.7 fusion.52
  201.2 0.7 multiply_subtract_fusion
  (31 shorter events, 0.2 us)
Async XLA Ops:
  0.6 84.5 %copy-start = (bf16[24,240,240]{2,1,0:T(8,128)(2,1)S(1)}, bf16[24,240,240]{2,1,0:T(8,128)(2,1)}, u32[]{:S(2)}) copy-start(bf16[24,240,240]{2,1,0:T(8,128)(2,1)} %param.14) | copy-start | bytes 8294404
  1.6 2.8 %copy-start.7 = (pred[64,4,1]{1,0,2:T(32,128)(4,1)}, pred[64,4,1]{1,0,2:T(32,128)(4,1)S(1)}, u32[]{:S(2)}) copy-start(pred[64,4,1]{1,0,2:T(32,128)(4,1)S(1)} %fusion.46) | copy-start | bytes 772
  6.4 22.3 %all-to-all-start = ((f32[32,1,1]{2,1,0:T(1,128)}), f32[32,1,1]{2,1,0:T(1,128)S(1)}, u32[]{:S(2)}, u32[]{:S(2)}) async-start(f32[32,1,1]{2,1,0:T(1,128)} %broadcast_in_dim.21), calls=%async_computation | async-start | bytes 32768 | tf_op jit(solution)/shard_map/all_to_all | solution.py:34
  30.5 16.2 %all-to-all-start.1 = ((f32[16,1,1]{2,1,0:T(1,128)}), f32[16,1,1]{2,1,0:T(1,128)S(1)}, u32[]{:S(2)}, u32[]{:S(2)}) async-start(f32[16,1,1]{2,1,0:T(1,128)} %broadcast_in_dim.22), calls=%async_computation.1 | async-start | bytes 16384 | tf_op jit(solution)/shard_map/all_to_all | solution.py:34
  48.1 5.3 %collective-permute-start = (f32[4,16,240]{2,1,0:T(8,128)S(1)}, f32[4,16,240]{2,1,0:T(8,128)S(1)}, u32[]{:S(2)}, u32[]{:S(2)}) collective-permute-start(f32[4,16,240]{2,1,0:T(8,128)S(1)} %broadcast_divide_fusion), channel_id=1, source_target_pairs={{0,32},{32,64},{64,96},{96,128},{128,160},{160,192},{192,224},{224... | collective-permute-start | bytes 184328 | tf_op jit(solution)/shard_map/ppermute | solution.py:23
  50.8 5.6 %collective-permute-start.1 = (f32[4,16,240]{2,1,0:T(8,128)S(1)}, f32[4,16,240]{2,1,0:T(8,128)S(1)}, u32[]{:S(2)}, u32[]{:S(2)}) collective-permute-start(f32[4,16,240]{2,1,0:T(8,128)S(1)} %broadcast_divide_fusion), channel_id=1, source_target_pairs={{32,0},{64,32},{96,64},{128,96},{160,128},{192,160},{224,192},{256... | collective-permute-start | bytes 184328 | tf_op jit(solution)/shard_map/ppermute | solution.py:25
  56.4 4.4 %copy-start.3 = (f32[4,16,240]{2,1,0:T(8,128)}, f32[4,16,240]{2,1,0:T(8,128)S(1)}, u32[]{:S(2)}) copy-start(f32[4,16,240]{2,1,0:T(8,128)S(1)} %collective-permute-done.1) | copy-start | bytes 184324
  56.4 4.3 %collective-permute-start.2 = (f32[12,4,240]{2,1,0:T(4,128)S(1)}, f32[12,4,240]{2,1,0:T(4,128)S(1)}, u32[]{:S(2)}, u32[]{:S(2)}) collective-permute-start(f32[12,4,240]{2,1,0:T(4,128)S(1)} %get-tuple-element.12), channel_id=1, source_target_pairs={{0,1},{1,2},{2,3},{3,4},{4,5},{5,6},{6,7},{7,8},{8,9},{9,10},{10,1... | collective-permute-start | bytes 138248 | tf_op jit(solution)/shard_map/ppermute | solution.py:23
  58.7 4.8 %collective-permute-start.3 = (f32[12,4,240]{2,1,0:T(4,128)S(1)}, f32[12,4,240]{2,1,0:T(4,128)S(1)}, u32[]{:S(2)}, u32[]{:S(2)}) collective-permute-start(f32[12,4,240]{2,1,0:T(4,128)S(1)} %get-tuple-element.13), channel_id=1, source_target_pairs={{1,0},{2,1},{3,2},{4,3},{5,4},{6,5},{7,6},{8,7},{9,8},{10,9},{11,1... | collective-permute-start | bytes 138248 | tf_op jit(solution)/shard_map/ppermute | solution.py:25
  64.4 16.1 %copy-start.5 = (s32[4,16,64]{2,1,0:T(8,128)S(1)}, s32[4,16,64]{2,1,0:T(8,128)}, u32[]{:S(2)}) copy-start(s32[4,16,64]{2,1,0:T(8,128)} %param.12) | copy-start | bytes 49156
  64.4 16.1 %copy-start.6 = (pred[64,64]{1,0:T(8,128)(4,1)S(1)}, pred[64,64]{1,0:T(8,128)(4,1)}, u32[]{:S(2)}) copy-start(pred[64,64]{1,0:T(8,128)(4,1)} %compare_and_fusion) | copy-start | bytes 12292
  80.5 5.7 %copy-start.1 = (f32[4,240,240]{2,1,0:T(8,128)S(1)}, f32[4,240,240]{2,1,0:T(8,128)}, u32[]{:S(2)}) copy-start(f32[4,240,240]{2,1,0:T(8,128)} %param.15) | copy-start | bytes 2764804
  80.5 6.7 %copy-start.8 = (pred[64,4,1]{1,0,2:T(32,128)(4,1)S(1)}, pred[64,4,1]{1,0,2:T(32,128)(4,1)}, u32[]{:S(2)}) copy-start(pred[64,4,1]{1,0,2:T(32,128)(4,1)} %copy-done.7) | copy-start | bytes 772
  106.6 12.8 %all-to-all-start.3 = ((f32[16,1,2]{2,1,0:T(1,128)}), f32[16,1,2]{2,1,0:T(1,128)S(1)}, u32[]{:S(2)}, u32[]{:S(2)}) async-start(f32[16,1,2]{2,1,0:T(1,128)} %broadcast_in_dim.24), calls=%async_computation.3 | async-start | bytes 16384 | tf_op jit(solution)/shard_map/all_to_all | solution.py:34
  123.2 4.6 %collective-permute-start.4 = (f32[4,16,240]{2,1,0:T(8,128)S(1)}, f32[4,16,240]{2,1,0:T(8,128)S(1)}, u32[]{:S(2)}, u32[]{:S(2)}) collective-permute-start(f32[4,16,240]{2,1,0:T(8,128)S(1)} %get-tuple-element.8), channel_id=1, source_target_pairs={{0,32},{32,64},{64,96},{96,128},{128,160},{160,192},{192,224},{224... | collective-permute-start | bytes 184328 | tf_op jit(solution)/shard_map/ppermute | solution.py:23
  125.9 5.6 %collective-permute-start.5 = (f32[4,16,240]{2,1,0:T(8,128)S(1)}, f32[4,16,240]{2,1,0:T(8,128)S(1)}, u32[]{:S(2)}, u32[]{:S(2)}) collective-permute-start(f32[4,16,240]{2,1,0:T(8,128)S(1)} %get-tuple-element.8), channel_id=1, source_target_pairs={{32,0},{64,32},{96,64},{128,96},{160,128},{192,160},{224,192},{256... | collective-permute-start | bytes 184328 | tf_op jit(solution)/shard_map/ppermute | solution.py:25
  131.5 3.6 %collective-permute-start.6 = (f32[12,4,240]{2,1,0:T(4,128)S(1)}, f32[12,4,240]{2,1,0:T(4,128)S(1)}, u32[]{:S(2)}, u32[]{:S(2)}) collective-permute-start(f32[12,4,240]{2,1,0:T(4,128)S(1)} %get-tuple-element.10), channel_id=1, source_target_pairs={{0,1},{1,2},{2,3},{3,4},{4,5},{5,6},{6,7},{7,8},{8,9},{9,10},{10,1... | collective-permute-start | bytes 138248 | tf_op jit(solution)/shard_map/ppermute | solution.py:23
  133.7 4.8 %collective-permute-start.7 = (f32[12,4,240]{2,1,0:T(4,128)S(1)}, f32[12,4,240]{2,1,0:T(4,128)S(1)}, u32[]{:S(2)}, u32[]{:S(2)}) collective-permute-start(f32[12,4,240]{2,1,0:T(4,128)S(1)} %get-tuple-element.11), channel_id=1, source_target_pairs={{1,0},{2,1},{3,2},{4,3},{5,4},{6,5},{7,6},{8,7},{9,8},{10,9},{11,1... | collective-permute-start | bytes 138248 | tf_op jit(solution)/shard_map/ppermute | solution.py:25
  154.7 5.7 %copy-start.2 = (f32[4,240,240]{2,1,0:T(8,128)S(1)}, f32[4,240,240]{2,1,0:T(8,128)}, u32[]{:S(2)}) copy-start(f32[4,240,240]{2,1,0:T(8,128)} %param.15) | copy-start | bytes 2764804
  154.7 6.7 %copy-start.9 = (pred[64,4,1]{1,0,2:T(32,128)(4,1)S(1)}, pred[64,4,1]{1,0,2:T(32,128)(4,1)}, u32[]{:S(2)}) copy-start(pred[64,4,1]{1,0,2:T(32,128)(4,1)} %copy-done.7) | copy-start | bytes 772
  159.4 41.8 %copy-start.4 = (f32[4,16,240]{2,1,0:T(8,128)S(1)}, f32[4,16,240]{2,1,0:T(8,128)}, u32[]{:S(2)}) copy-start(f32[4,16,240]{2,1,0:T(8,128)} %get-tuple-element.9) | copy-start | bytes 184324
  182.0 12.8 %all-to-all-start.5 = ((f32[16,1,3]{2,1,0:T(1,128)}), f32[16,1,3]{2,1,0:T(1,128)S(1)}, u32[]{:S(2)}, u32[]{:S(2)}) async-start(f32[16,1,3]{2,1,0:T(1,128)} %broadcast_in_dim.26), calls=%async_computation.5 | async-start | bytes 16384 | tf_op jit(solution)/shard_map/all_to_all | solution.py:34
where the time goes:
time: 203 us; the launch traced here: 202 us
  starting transfers between devices  50.8 us (25%)
  waiting for transfers between devices  40.9 us (20%)
  local copies, waits for them, and re-layouts  38.2 us (19%)
  blocking collectives  32.2 us (16%)
  matrix products  17.3 us (9%)
  other arithmetic  12.6 us (6%)
  between operations  9.86 us (5%)
    all_to_all x4, starting transfers between devices, copy_for_each(): lax.all_to_all(jnp.broadcast_to(shard[None], (devices, *shard.shape)), ax...  34.5 us
    all_to_all x2, blocking collectives, copy_for_each(): lax.all_to_all(jnp.broadcast_to(shard[None], (devices, *shard.shape)), ax...  32.2 us
    gather x2, local copies, waits for them, and re-layouts, translate(): picked = jnp.take(flattened, targets, axis=0)  32.1 us
    all_to_all x4, waiting for transfers between devices, copy_for_each(): lax.all_to_all(jnp.broadcast_to(shard[None], (devices, *shard.shape)), ax...  28 us
    ppermute x4, waiting for transfers between devices, with_halo(): lax.ppermute(head, axis, [((i + 1) % count, i) for i in range(ends)])  12.9 us
    ppermute x4, starting transfers between devices, with_halo(): lax.ppermute(tail, axis, [(i, (i + 1) % count) for i in range(ends)])  9.92 us
    dot_general x2, matrix products, translate(): jnp.einsum('isk,isc->kic', chosen, picked, precision=lax.Precision.HIGHEST)  9.27 us
    ppermute x4, starting transfers between devices, with_halo(): lax.ppermute(head, axis, [((i + 1) % count, i) for i in range(ends)])  6.43 us
  transfers between devices with their start and end apart: 12, of which 8 were waited for; matrix products, arithmetic and copies ran while one was open for 1% of the time, Pallas kernels for 0%

commit v1 on v0

v1 whole, which is shorter than its diff:
```python
import functools

import jax
import jax.numpy as jnp
from jax import lax
from jax.experimental import pallas as pl
from jax.experimental.pallas import tpu as pltpu
from jax.sharding import PartitionSpec as P

MESH = pl.DeviceIdType.MESH
HALO = 4
STRIDE = 2 * HALO + 1
LANES = 256
EPSILON = 1e-06
F32, BF16 = jnp.float32, jnp.bfloat16

PIECES = (
    (1, 0, 0, 0, 64),
    (-1, 0, 0, 128, 64),
    (0, 1, 2, 16, 16),
    (1, 1, 2, 0, 16),
    (-1, 1, 2, 32, 16),
    (0, -1, 1, 64, 16),
    (1, -1, 1, 48, 16),
    (-1, -1, 1, 80, 16),
)


def nt(a, b):
    return lax.dot_general(a, b, (((1,), (1,)), ((), ())), preferred_element_type=F32)


def nn(a, b):
    return lax.dot_general(a, b, (((1,), (0,)), ((), ())), preferred_element_type=F32)


def split(x):
    hi = x.astype(BF16)
    return hi, (x - hi.astype(F32)).astype(BF16)


def iota(shape, dim):
    return lax.broadcasted_iota(jnp.int32, shape, dim)


def kernel(
    ngx, ngy, inc_ref, kinds_ref, codes_ref, ops_ref, valid_ref, trans_hbm, tmat_hbm,
    sol_ref, res_ref,
    trans_v, tmat_v, tmhi, tmlo, tt, counts, grouped, mid, side, edge, vhi, vlo,
    one_out, one_in, two_out, two_in,
    load_sem, halo_send, halo_recv, ar_send, ar_recv,
):
    gx, gy = lax.axis_index("gx"), lax.axis_index("gy")
    rows, cols, coeffs = inc_ref.shape
    spheres = rows * cols
    slots = codes_ref.shape[2]
    count_ops, kinds_n = trans_v.shape[0], tmat_v.shape[0]

    def device(dx, dy):
        return (lax.rem(gx + (dx + ngx), ngx), lax.rem(gy + (dy + ngy), ngy))

    load_tm = pltpu.make_async_copy(tmat_hbm, tmat_v, load_sem.at[0])
    load_tm.start()
    load_tr = pltpu.make_async_copy(trans_hbm, trans_v, load_sem.at[1])
    load_tr.start()

    barrier = pltpu.get_barrier_semaphore()
    greeted = 0
    for dx, dy in [(0, d) for d in range(1, ngy)] + [(d, 0) for d in range(1, ngx)] + [
        (1, 1), (1, -1), (-1, 1), (-1, -1)
    ]:
        pl.semaphore_signal(barrier, inc=1, device_id=device(dx, dy), device_id_type=MESH)
        greeted += 1

    lane = iota((spheres, LANES), 1)
    eye = iota((cols, cols), 0) == iota((cols, cols), 1)
    kind_col = jnp.concatenate(
        [
            jnp.sum(
                jnp.where(eye, jnp.broadcast_to(kinds_ref[r : r + 1, :], (cols, cols)), 0).astype(F32),
                axis=1, keepdims=True,
            )
            for r in range(rows)
        ],
        axis=0,
    )

    def apply_kinds(u):
        total = None
        for p in range(kinds_n):
            hi, lo = split(jnp.where(kind_col == p, u, 0.0))
            term = nt(hi, tmhi[p]) + nt(lo, tmhi[p]) + nt(hi, tmlo[p])
            total = term if total is None else total + term
        return total

    def set_field(h, u):
        mid[h, spheres : 2 * spheres, :] = jnp.zeros((spheres, LANES), F32)
        mid[h, spheres : 2 * spheres, :coeffs] = u

        for r in range(rows):
            for e, c in ((0, 0), (1, cols - HALO)):
                edge[h, e, HALO * r : HALO * (r + 1), :] = mid[
                    h, spheres + cols * r + c : spheres + cols * r + c + HALO, :
                ]

    def exchange(h):
        copies = []
        for n, (dx, dy, source, first, count) in enumerate(PIECES):
            if source == 0:
                src, dst = mid.at[h, pl.ds(spheres, spheres)], mid.at[h, pl.ds(first, count)]
            else:
                src, dst = edge.at[h, source - 1], side.at[h, pl.ds(first, count)]
            copy = pltpu.make_async_remote_copy(
                src_ref=src, dst_ref=dst, send_sem=halo_send.at[h, n], recv_sem=halo_recv.at[h, n],
                device_id=device(dx, dy), device_id_type=MESH,
            )
            copy.start()
            copies.append(copy)
        return copies

    load_tm.wait()
    for p in range(kinds_n):
        hi, lo = split(tmat_v[p])
        tmhi[p] = hi
        tmlo[p] = lo
    set_field(0, apply_kinds(inc_ref[...].reshape(spheres, coeffs)))
    pl.semaphore_wait(barrier, greeted)
    flights = exchange(0)

    codes = codes_ref[...].reshape(spheres, slots)
    sphere = iota((spheres, slots), 0)
    row, col = sphere >> 4, sphere & 15
    step_x = (codes * 57) >> 9
    ext_x = row + step_x
    ext_y = col + codes - STRIDE * step_x
    target = jnp.where(
        ext_y < HALO,
        144 + HALO * ext_x + ext_y,
        jnp.where(ext_y < HALO + cols, cols * step_x + ext_y - HALO, 172 + HALO * ext_x + ext_y),
    )
    at_x = gx * rows + ext_x - HALO
    at_y = gy * cols + ext_y - HALO
    inside = (at_x >= 0) & (at_x < ngx * rows) & (at_y >= 0) & (at_y < ngy * cols)
    inside = inside & (valid_ref[...].reshape(spheres, slots) == 1)
    key = jnp.where(inside, row * count_ops + ops_ref[...].reshape(spheres, slots), -1)
    target = jnp.concatenate([target[cols * r : cols * (r + 1)] for r in range(rows)], axis=1)
    key = jnp.concatenate([key[cols * r : cols * (r + 1)] for r in range(rows)], axis=1)
    for c in range(cols):
        left = (iota((rows * count_ops, LANES), 0) == key[c : c + 1, :]).astype(F32).astype(BF16)
        right = (iota((LANES, LANES), 0) == target[c : c + 1, :]).astype(F32).astype(BF16)
        tally = nt(left, right)
        for r in range(rows):
            piece = tally[count_ops * r : count_ops * (r + 1)]
            for half in range(2):
                counts[half, pl.ds(r * cols * count_ops + c, count_ops, stride=cols), :] = piece[
                    :, 128 * half : 128 * (half + 1)
                ]

    load_tr.wait()
    unit = (iota((LANES, coeffs), 0) == iota((LANES, coeffs), 1)).astype(F32).astype(BF16)
    for k in range(count_ops):
        tt[k, :, :coeffs] = nt(unit, trans_v[k]).astype(BF16)

    def couple(h, copies):
        for copy in copies:
            copy.wait_recv()
        hi, lo = split(mid[h])
        vhi[: 3 * spheres], vlo[: 3 * spheres] = hi, lo
        hi, lo = split(side[h])
        vhi[3 * spheres :], vlo[3 * spheres :] = hi, lo
        tail = jnp.zeros((16, LANES), BF16)
        per_row = cols * count_ops
        for r in range(rows):
            table = jnp.concatenate(
                [counts[half, per_row * r : per_row * (r + 1), :].astype(BF16) for half in range(2)], axis=1
            )
            near = [
                jnp.concatenate([v[cols * r : cols * (r + STRIDE)], v[3 * spheres :], tail], axis=0)
                for v in (vhi, vlo)
            ]
            grouped[per_row * r : per_row * (r + 1), :] = nn(table, near[0]) + nn(table, near[1])
        total = None
        for k in range(count_ops):
            part = jnp.concatenate(
                [grouped[per_row * r + cols * k : per_row * r + cols * (k + 1), :] for r in range(rows)], axis=0
            )
            hi, lo = split(part)
            term = nn(jnp.concatenate([hi, lo], axis=0), tt[k])
            total = term if total is None else total + term
        moved = total[:spheres] + total[spheres:]
        return apply_kinds(moved[:, :coeffs])

    first_flights = flights
    set_field(1, couple(0, flights))
    flights = exchange(1)
    second = couple(1, flights)

    base = mid[0, spheres : 2 * spheres, :coeffs]
    once = mid[1, spheres : 2 * spheres, :coeffs]

    def inner(a, b):
        return jnp.sum(jnp.sum(a * b, axis=0, keepdims=True), axis=1, keepdims=True)

    products = (
        inner(base, base), inner(base, once), inner(once, once),
        inner(base, second), inner(once, second), inner(second, second),
    )
    slot = iota((1, 128), 1)
    packed = jnp.zeros((1, 128), F32)
    for n, value in enumerate(products):
        packed = jnp.where(slot == n, value, packed)

    def all_sum(n, value, out, into, peers):
        out[...] = value
        for d, peer in enumerate(peers):
            pltpu.make_async_remote_copy(
                src_ref=out, dst_ref=into.at[d], send_sem=ar_send.at[n], recv_sem=ar_recv.at[n],
                device_id=peer, device_id_type=MESH,
            ).start()
        pltpu.make_async_copy(into, into, ar_recv.at[n]).wait()
        total = value
        for d in range(len(peers)):
            total = total + into[d]
        return total

    packed = all_sum(0, packed, one_out, one_in, [device(0, d) for d in range(1, ngy)])
    packed = all_sum(1, packed, two_out, two_in, [device(d, 0) for d in range(1, ngx)])

    def entry(n):
        return jnp.sum(jnp.where(slot == n, packed, 0.0), axis=1, keepdims=True)

    g00, g01, g11, g02, g12, g22 = [entry(n) for n in range(6)]
    gram = ((g00, g01, g02), (g01, g11, g12), (g02, g12, g22))

    def pair(a, b):
        total = None
        for i in range(3):
            for j in range(3):
                if a[i] is not None and b[j] is not None:
                    term = a[i] * b[j] * gram[i][j]
                    total = term if total is None else total + term
        return total

    beta2 = g00 + EPSILON
    beta = jnp.sqrt(beta2)
    ib = 1.0 / beta
    shift = (g01 + EPSILON) * ib * ib
    h11 = (g00 - g01) * ib * ib
    rest = (shift * ib, -ib, None)
    h21 = jnp.sqrt(jnp.maximum(pair(rest, rest), 0.0) + EPSILON)
    q = ib / h21
    v1 = (ib, None, None)
    v2 = (shift * q, -q, None)
    m2 = (shift * q, -(1.0 + shift) * q, q)
    h12 = pair(m2, v1)
    left = (m2[0] - h12 * ib, m2[1], m2[2])
    h22 = pair(left, v2)
    left = (left[0] - h22 * v2[0], left[1] - h22 * v2[1], left[2])
    h32 = jnp.sqrt(jnp.maximum(pair(left, left), 0.0) + EPSILON)
    aa = h11 * h11 + h21 * h21
    ab = h11 * h12 + h21 * h22
    bb = h12 * h12 + h22 * h22 + h32 * h32
    ra, rb = beta * h11, beta * h12
    determ = aa * bb - ab * ab
    y1 = (bb * ra - ab * rb) / determ
    y2 = (aa * rb - ab * ra) / determ
    s0 = y1 * ib + y2 * v2[0]
    s1 = y2 * v2[1]
    r0 = 1.0 - s0
    r1 = y1 * ib - y2 * m2[1]
    r2 = -y2 * q
    sol_ref[...] = (s0 * base + s1 * once).reshape(rows, cols, coeffs)
    res_ref[...] = (r0 * base + r1 * once + r2 * second).reshape(rows, cols, coeffs)

    for copy in first_flights + flights:
        copy.wait_send()
    pltpu.make_async_copy(one_in, one_in, ar_send.at[0]).wait()
    pltpu.make_async_copy(two_in, two_in, ar_send.at[1]).wait()


def solution(mesh):
    ngx, ngy = mesh.shape["gx"], mesh.shape["gy"]

    def body(incident, sphere_kinds, pair_codes, operators, pair_valid, translations, tmatrices):
        rows, cols, coeffs = incident.shape
        spheres = rows * cols
        count_ops, kinds_n = translations.shape[0], tmatrices.shape[0]
        vmem = pl.BlockSpec(memory_space=pltpu.VMEM)
        hbm = pl.BlockSpec(memory_space=pltpu.HBM)
        return pl.pallas_call(
            functools.partial(kernel, ngx, ngy),
            out_shape=(jax.ShapeDtypeStruct(incident.shape, F32),) * 2,
            in_specs=[vmem] * 5 + [hbm] * 2,
            out_specs=(vmem, vmem),
            scratch_shapes=[
                pltpu.VMEM(translations.shape, BF16),
                pltpu.VMEM(tmatrices.shape, F32),
                pltpu.VMEM(tmatrices.shape, BF16),
                pltpu.VMEM(tmatrices.shape, BF16),
                pltpu.VMEM((count_ops, LANES, LANES), BF16),
                pltpu.VMEM((2, spheres * count_ops, 128), F32),
                pltpu.VMEM((spheres * count_ops, LANES), F32),
                pltpu.VMEM((2, 3 * spheres, LANES), F32),
                pltpu.VMEM((2, 96, LANES), F32),
                pltpu.VMEM((2, 2, 16, LANES), F32),
                pltpu.VMEM((3 * spheres + 96, LANES), BF16),
                pltpu.VMEM((3 * spheres + 96, LANES), BF16),
                pltpu.VMEM((1, 128), F32),
                pltpu.VMEM((ngy - 1, 1, 128), F32),
                pltpu.VMEM((1, 128), F32),
                pltpu.VMEM((ngx - 1, 1, 128), F32),
                pltpu.SemaphoreType.DMA((2,)),
                pltpu.SemaphoreType.DMA((2, len(PIECES))),
                pltpu.SemaphoreType.DMA((2, len(PIECES))),
                pltpu.SemaphoreType.DMA((2,)),
                pltpu.SemaphoreType.DMA((2,)),
            ],
            compiler_params=pltpu.CompilerParams(collective_id=0, has_side_effects=True),
        )(incident, sphere_kinds, pair_codes, operators, pair_valid, translations, tmatrices)

    here, line, table = P("gx", "gy", None), P("gx", "gy"), P()
    return jax.shard_map(
        body, mesh=mesh, in_specs=(here, line, here, here, here, table, table), out_specs=(here, here), check_vma=False
    )
```

time: 203 us -> 46 us (0.23)
  starting transfers between devices: 50.8 us -> 0 us
  Pallas kernels: 0 us -> 42.2 us
  waiting for transfers between devices: 40.9 us -> 0 us
  local copies, waits for them, and re-layouts: 38.2 us -> 2.95 us
  blocking collectives: 32.2 us -> 0 us
  matrix products: 17.3 us -> 0 us
  other arithmetic: 12.6 us -> 0 us
  between operations: 9.86 us -> 0.64 us
    pallas_call x0 -> x1, Pallas kernels: none -> 42.2 us  [body(): pl.pallas_call(functools.partial(kernel, ngx, ngy), out_shape=(jax.ShapeD...]
    all_to_all x4 -> x0, starting transfers between devices: 34.5 us -> none  [copy_for_each(): lax.all_to_all(jnp.broadcast_to(shard[None], (devices, *shard.shape)), ax...]
    all_to_all x2 -> x0, blocking collectives: 32.2 us -> none  [copy_for_each(): lax.all_to_all(jnp.broadcast_to(shard[None], (devices, *shard.shape)), ax...]
    gather x2 -> x0, local copies, waits for them, and re-layouts: 32.1 us -> none  [translate(): picked = jnp.take(flattened, targets, axis=0)]
    all_to_all x4 -> x0, waiting for transfers between devices: 28 us -> none  [copy_for_each(): lax.all_to_all(jnp.broadcast_to(shard[None], (devices, *shard.shape)), ax...]
    dot_general x10 -> x0, matrix products: 17.3 us -> none  [the longest x2 9.27 us: translate(): jnp.einsum('isk,isc->kic', chosen, picked, precision=lax.Precision.HIGHEST)]
    ppermute x8 -> x0, starting transfers between devices: 16.3 us -> none  [the longest x4 9.92 us: with_halo(): lax.ppermute(tail, axis, [(i, (i + 1) % count) for i in range(ends)])]
    ppermute x8 -> x0, waiting for transfers between devices: 12.9 us -> none  [the longest x4 12.9 us: with_halo(): lax.ppermute(head, axis, [((i + 1) % count, i) for i in range(ends)])]
  transfers between devices with their start and end apart: 12 -> 0, of which waited for: 8 -> 0; matrix products, arithmetic and copies ran while one was open for 1% -> 0% of each run, Pallas kernels for 0% -> 0%
where the time goes in v1:
time: 46 us; the launch traced here: 45.7 us
  Pallas kernels  42.2 us (92%)
  local copies, waits for them, and re-layouts  2.95 us (6%)
  between operations  0.64 us (1%)
    pallas_call x1, Pallas kernels, body(): pl.pallas_call(functools.partial(kernel, ngx, ngy), out_shape=(jax.ShapeD...  42.2 us
    unnamed x2, local copies, waits for them, and re-layouts  2.95 us

profile of v1, /device:TPU:1, one launch (start us, length us, event | category | flops | bytes accessed | tf_op | source)
XLA Modules:
  0.0 45.7 jit_solution(9144297794524652298)
XLA Ops:
  0.6 42.2 %shard_map.86 = (f32[4,16,240]{2,1,0:T(8,128)}, f32[4,16,240]{2,1,0:T(8,128)}) custom-call(f32[4,16,240]{2,1,0:T(8,128)} %inc_ref.1, s32[4,16]{1,0:T(4,128)} %kinds_ref.1, s32[4,16,64]{2,1,0:T(8,128)} %codes_ref.1, s32[4,16,64]{2,1,0:T(8,128)} %ops_ref.1, s32[4,16,64]{2,1,0:T(8,128)} %valid_ref.1, bf16[24,240,240]{2,1,0:T(8,128)(2,1)} %trans_hbm.1, ...), custom_call_target="tpu_custom_call" | custom-call | tf_op jit(solution)/shard_map/pallas_call | solution.py:290
  42.8 1.5 %copy.11 = f32[4,16,240]{2,1,0:T(8,128)} copy(f32[4,16,240]{2,1,0:T(8,128)} %get-tuple-element.4) | data formatting | bytes 122880
  44.3 1.5 %copy.12 = f32[4,16,240]{2,1,0:T(8,128)} copy(f32[4,16,240]{2,1,0:T(8,128)} %get-tuple-element.5) | data formatting | bytes 122880

commit v2 on v1

--- a/solution.py
+++ b/solution.py
@@ -15,14 +15,14 @@
 F32, BF16 = jnp.float32, jnp.bfloat16
 
 PIECES = (
+    (1, 1, 2, 0, 16),
+    (-1, 1, 2, 32, 16),
+    (1, -1, 1, 48, 16),
+    (-1, -1, 1, 80, 16),
+    (0, 1, 2, 16, 16),
+    (0, -1, 1, 64, 16),
     (1, 0, 0, 0, 64),
     (-1, 0, 0, 128, 64),
-    (0, 1, 2, 16, 16),
-    (1, 1, 2, 0, 16),
-    (-1, 1, 2, 32, 16),
-    (0, -1, 1, 64, 16),
-    (1, -1, 1, 48, 16),
-    (-1, -1, 1, 80, 16),
 )
 
 
@@ -43,12 +43,21 @@
     return lax.broadcasted_iota(jnp.int32, shape, dim)
 
 
+def spread(n):
+    steps, d = [], 1
+    while d < n // 2:
+        steps.append(d)
+        d *= 2
+    return steps
+
+
 def kernel(
-    ngx, ngy, inc_ref, kinds_ref, codes_ref, ops_ref, valid_ref, trans_hbm, tmat_hbm,
-    sol_ref, res_ref,
-    trans_v, tmat_v, tmhi, tmlo, tt, counts, grouped, mid, side, edge, vhi, vlo,
+    ngx, ngy, inc_hbm, kinds_hbm, codes_hbm, ops_hbm, valid_hbm, trans_hbm, tmat_hbm,
+    state, sums,
+    inc_ref, kinds_ref, codes_ref, ops_ref, valid_ref, trans_v, tmat_v,
+    tmhi, tmlo, tmhi_t, tmlo_t, masks, tt, counts, grouped, mid, side, edge, vhi, vlo,
     one_out, one_in, two_out, two_in,
-    load_sem, halo_send, halo_recv, ar_send, ar_recv,
+    load_sem, halo_send, halo_recv, ar_send, ar_recv, spread_sem,
 ):
     gx, gy = lax.axis_index("gx"), lax.axis_index("gy")
     rows, cols, coeffs = inc_ref.shape
@@ -58,20 +67,34 @@
 
     def device(dx, dy):
         return (lax.rem(gx + (dx + ngx), ngx), lax.rem(gy + (dy + ngy), ngy))
-
-    load_tm = pltpu.make_async_copy(tmat_hbm, tmat_v, load_sem.at[0])
-    load_tm.start()
-    load_tr = pltpu.make_async_copy(trans_hbm, trans_v, load_sem.at[1])
-    load_tr.start()
-
     barrier = pltpu.get_barrier_semaphore()
-    greeted = 0
-    for dx, dy in [(0, d) for d in range(1, ngy)] + [(d, 0) for d in range(1, ngx)] + [
-        (1, 1), (1, -1), (-1, 1), (-1, -1)
-    ]:
+    for dx, dy, _, _, _ in PIECES:
         pl.semaphore_signal(barrier, inc=1, device_id=device(dx, dy), device_id_type=MESH)
-        greeted += 1
-
+    loads = []
+    for n, (src, dst) in enumerate((
+        (tmat_hbm, tmat_v), (inc_hbm, inc_ref), (kinds_hbm, kinds_ref), (codes_hbm, codes_ref),
+        (ops_hbm, ops_ref), (valid_hbm, valid_ref), (trans_hbm, trans_v),
+    )):
+        loads.append(pltpu.make_async_copy(src, dst, load_sem.at[n]))
+        loads[-1].start()
+
+    rounds = [[(0, d) for d in spread(ngy)], [(d, 0) for d in spread(ngx)]]
+
+    def tell(n):
+        for axis, steps in enumerate(rounds):
+            if n < len(steps):
+                dx, dy = steps[n]
+                for sign in (1, -1):
+                    pl.semaphore_signal(
+                        spread_sem.at[axis, n], inc=1, device_id=device(sign * dx, sign * dy), device_id_type=MESH
+                    )
+
+    def hear(n):
+        for axis, steps in enumerate(rounds):
+            if n < len(steps):
+                pl.semaphore_wait(spread_sem.at[axis, n], 2)
+    for n in range(3):
+        loads[n].wait()
     lane = iota((spheres, LANES), 1)
     eye = iota((cols, cols), 0) == iota((cols, cols), 1)
     kind_col = jnp.concatenate(
@@ -85,7 +108,7 @@
         axis=0,
     )
 
-    def apply_kinds(u):
+    def source_of(u):
         total = None
         for p in range(kinds_n):
             hi, lo = split(jnp.where(kind_col == p, u, 0.0))
@@ -93,10 +116,19 @@
             total = term if total is None else total + term
         return total
 
+    def apply_kinds(u):
+        hi, lo = split(u)
+        both = jnp.concatenate([hi, lo], axis=0)
+        wide, fine = None, None
+        for p in range(kinds_n):
+            chosen = both * masks[p]
+            term, more = nn(chosen, tmhi_t[p]), nn(chosen[:spheres], tmlo_t[p])
+            wide, fine = (term, more) if wide is None else (wide + term, fine + more)
+        return jnp.where(lane < coeffs, wide[:spheres] + wide[spheres:] + fine, 0.0)
+
     def set_field(h, u):
-        mid[h, spheres : 2 * spheres, :] = jnp.zeros((spheres, LANES), F32)
-        mid[h, spheres : 2 * spheres, :coeffs] = u
-
+        mid[h, spheres : 2 * spheres, :] = u
+        state[h] = u
         for r in range(rows):
             for e, c in ((0, 0), (1, cols - HALO)):
                 edge[h, e, HALO * r : HALO * (r + 1), :] = mid[
@@ -118,15 +150,18 @@
             copies.append(copy)
         return copies
 
-    load_tm.wait()
     for p in range(kinds_n):
         hi, lo = split(tmat_v[p])
         tmhi[p] = hi
         tmlo[p] = lo
-    set_field(0, apply_kinds(inc_ref[...].reshape(spheres, coeffs)))
-    pl.semaphore_wait(barrier, greeted)
+    state[0] = jnp.zeros((spheres, LANES), F32)
+    state[0, :, :coeffs] = source_of(inc_ref[...].reshape(spheres, coeffs))
+    set_field(0, state[0])
+    pl.semaphore_wait(barrier, len(PIECES))
     flights = exchange(0)
-
+    tell(0)
+    for n in range(3, 6):
+        loads[n].wait()
     codes = codes_ref[...].reshape(spheres, slots)
     sphere = iota((spheres, slots), 0)
     row, col = sphere >> 4, sphere & 15
@@ -156,11 +191,19 @@
                     :, 128 * half : 128 * (half + 1)
                 ]
 
-    load_tr.wait()
+    loads[6].wait()
+    hear(0)
+    tell(1)
     unit = (iota((LANES, coeffs), 0) == iota((LANES, coeffs), 1)).astype(F32).astype(BF16)
     for k in range(count_ops):
         tt[k, :, :coeffs] = nt(unit, trans_v[k]).astype(BF16)
-
+    for p in range(kinds_n):
+        tmhi_t[p, :, :coeffs] = nt(unit, tmhi[p]).astype(BF16)
+        tmlo_t[p, :, :coeffs] = nt(unit, tmlo[p]).astype(BF16)
+        mask = jnp.where(jnp.broadcast_to(kind_col, (spheres, LANES)) == p, 1.0, 0.0)
+        masks[p] = jnp.concatenate([mask, mask], axis=0).astype(BF16)
+    hear(1)
+    tell(2)
     def couple(h, copies):
         for copy in copies:
             copy.wait_recv()
@@ -187,16 +230,19 @@
             hi, lo = split(part)
             term = nn(jnp.concatenate([hi, lo], axis=0), tt[k])
             total = term if total is None else total + term
-        moved = total[:spheres] + total[spheres:]
-        return apply_kinds(moved[:, :coeffs])
+        moved = jnp.where(lane < coeffs, total[:spheres] + total[spheres:], 0.0)
+        result = apply_kinds(moved)
+        return result
 
     first_flights = flights
-    set_field(1, couple(0, flights))
+    once = couple(0, flights)
+    set_field(1, once)
     flights = exchange(1)
+    hear(2)
+    tell(3)
     second = couple(1, flights)
-
-    base = mid[0, spheres : 2 * spheres, :coeffs]
-    once = mid[1, spheres : 2 * spheres, :coeffs]
+    state[2] = second
+    base, once = state[0], state[1]
 
     def inner(a, b):
         return jnp.sum(jnp.sum(a * b, axis=0, keepdims=True), axis=1, keepdims=True)
@@ -209,7 +255,6 @@
     packed = jnp.zeros((1, 128), F32)
     for n, value in enumerate(products):
         packed = jnp.where(slot == n, value, packed)
-
     def all_sum(n, value, out, into, peers):
         out[...] = value
         for d, peer in enumerate(peers):
@@ -223,8 +268,26 @@
             total = total + into[d]
         return total
 
-    packed = all_sum(0, packed, one_out, one_in, [device(0, d) for d in range(1, ngy)])
-    packed = all_sum(1, packed, two_out, two_in, [device(d, 0) for d in range(1, ngx)])
+    def far_first(n, inner):
+        def hops(d):
+            return min(d // inner, n // inner - d // inner) + min(d % inner, inner - d % inner)
+
+        return sorted(range(1, n), key=lambda d: -hops(d))
+    hear(3)
+    packed = all_sum(0, packed, one_out, one_in, [device(0, d) for d in far_first(ngy, 8)])
+    packed = all_sum(1, packed, two_out, two_in, [device(d, 0) for d in far_first(ngx, 2)])
+    sums[...] = packed
+    for copy in first_flights + flights:
+        copy.wait_send()
+    pltpu.make_async_copy(one_in, one_in, ar_send.at[0]).wait()
+    pltpu.make_async_copy(two_in, two_in, ar_send.at[1]).wait()
+
+
+def combine(state, sums, sol_ref, res_ref):
+    rows, cols, coeffs = sol_ref.shape
+    packed = sums[...]
+    slot = iota((1, 128), 1)
+    base, once, second = [state[n][:, :coeffs] for n in range(3)]
 
     def entry(n):
         return jnp.sum(jnp.where(slot == n, packed, 0.0), axis=1, keepdims=True)
@@ -272,11 +335,6 @@
     sol_ref[...] = (s0 * base + s1 * once).reshape(rows, cols, coeffs)
     res_ref[...] = (r0 * base + r1 * once + r2 * second).reshape(rows, cols, coeffs)
 
-    for copy in first_flights + flights:
-        copy.wait_send()
-    pltpu.make_async_copy(one_in, one_in, ar_send.at[0]).wait()
-    pltpu.make_async_copy(two_in, two_in, ar_send.at[1]).wait()
-
 
 def solution(mesh):
     ngx, ngy = mesh.shape["gx"], mesh.shape["gy"]
@@ -287,16 +345,17 @@
         count_ops, kinds_n = translations.shape[0], tmatrices.shape[0]
         vmem = pl.BlockSpec(memory_space=pltpu.VMEM)
         hbm = pl.BlockSpec(memory_space=pltpu.HBM)
-        return pl.pallas_call(
+        args = (incident, sphere_kinds, pair_codes, operators, pair_valid, translations, tmatrices)
+        state, sums = pl.pallas_call(
             functools.partial(kernel, ngx, ngy),
-            out_shape=(jax.ShapeDtypeStruct(incident.shape, F32),) * 2,
-            in_specs=[vmem] * 5 + [hbm] * 2,
+            out_shape=(pltpu.VMEM((3, spheres, LANES), F32), pltpu.VMEM((1, 128), F32)),
+            in_specs=[hbm] * 7,
             out_specs=(vmem, vmem),
-            scratch_shapes=[
-                pltpu.VMEM(translations.shape, BF16),
-                pltpu.VMEM(tmatrices.shape, F32),
-                pltpu.VMEM(tmatrices.shape, BF16),
-                pltpu.VMEM(tmatrices.shape, BF16),
+            scratch_shapes=[pltpu.VMEM(arg.shape, arg.dtype) for arg in args]
+            + [pltpu.VMEM(tmatrices.shape, BF16)] * 2
+            + [pltpu.VMEM((kinds_n, LANES, LANES), BF16)] * 2
+            + [
+                pltpu.VMEM((kinds_n, 2 * spheres, LANES), BF16),
                 pltpu.VMEM((count_ops, LANES, LANES), BF16),
                 pltpu.VMEM((2, spheres * count_ops, 128), F32),
                 pltpu.VMEM((spheres * count_ops, LANES), F32),
@@ -309,14 +368,22 @@
                 pltpu.VMEM((ngy - 1, 1, 128), F32),
                 pltpu.VMEM((1, 128), F32),
                 pltpu.VMEM((ngx - 1, 1, 128), F32),
-                pltpu.SemaphoreType.DMA((2,)),
+                pltpu.SemaphoreType.DMA((7,)),
                 pltpu.SemaphoreType.DMA((2, len(PIECES))),
                 pltpu.SemaphoreType.DMA((2, len(PIECES))),
                 pltpu.SemaphoreType.DMA((2,)),
                 pltpu.SemaphoreType.DMA((2,)),
+                pltpu.SemaphoreType.REGULAR((2, 4)),
             ],
             compiler_params=pltpu.CompilerParams(collective_id=0, has_side_effects=True),
-        )(incident, sphere_kinds, pair_codes, operators, pair_valid, translations, tmatrices)
+        )(*args)
+        state, sums = [pltpu.with_memory_space_constraint(x, pltpu.VMEM) for x in (state, sums)]
+        return pl.pallas_call(
+            combine,
+            out_shape=(jax.ShapeDtypeStruct(incident.shape, F32),) * 2,
+            in_specs=[vmem] * 2,
+            out_specs=(vmem, vmem),
+        )(state, sums)
 
     here, line, table = P("gx", "gy", None), P("gx", "gy"), P()
     return jax.shard_map(

time: 46 us -> 40.4 us (0.88)
  local copies, waits for them, and re-layouts: 2.95 us -> 0 us
  Pallas kernels: 42.2 us -> 39.7 us
    unnamed x2 -> x0, local copies, waits for them, and re-layouts: 2.95 us -> none
    pallas_call x1 -> x2, Pallas kernels: 42.2 us -> 39.7 us  [the longest x1 38.9 us: body(): pl.pallas_call(functools.partial(kernel, ngx, ngy), out_shape=(pltpu.VMEM...]
where the time goes in v2:
time: 40.4 us; the launch traced here: 40.3 us
  Pallas kernels  39.7 us (98%)
  between operations  0.64 us (2%)
    pallas_call x1, Pallas kernels, body(): pl.pallas_call(functools.partial(kernel, ngx, ngy), out_shape=(pltpu.VMEM...  38.9 us
    pallas_call x1, Pallas kernels, body(): pl.pallas_call(combine, out_shape=(jax.ShapeDtypeStruct(incident.shape, F...  0.83 us

profile of v2, /device:TPU:1, one launch (start us, length us, event | category | flops | bytes accessed | tf_op | source)
XLA Modules:
  0.0 40.3 jit_solution(10031955656829493403)
XLA Ops:
  0.6 38.9 %shard_map.86 = (f32[3,64,256]{2,1,0:T(8,128)S(1)}, f32[1,128]{1,0:T(1,128)S(1)}) custom-call(f32[4,16,240]{2,1,0:T(8,128)} %inc_hbm.1, s32[4,16]{1,0:T(4,128)} %kinds_hbm.1, s32[4,16,64]{2,1,0:T(8,128)} %codes_hbm.1, s32[4,16,64]{2,1,0:T(8,128)} %ops_hbm.1, s32[4,16,64]{2,1,0:T(8,128)} %valid_hbm.1, bf16[24,240,240]{2,1,0:T(8,128)(2,1)} %trans_hbm.1, ...), custom_call_target="tpu_custom_call" | custom-call | tf_op jit(solution)/shard_map/pallas_call | solution.py:349
  39.5 0.8 %shard_map.87 = (f32[4,16,240]{2,1,0:T(8,128)}, f32[4,16,240]{2,1,0:T(8,128)}) custom-call(f32[3,64,256]{2,1,0:T(8,128)S(1)} %get-tuple-element.4.state, f32[1,128]{1,0:T(1,128)S(1)} %get-tuple-element.5.sums), custom_call_target="tpu_custom_call" | custom-call | tf_op jit(solution)/shard_map/pallas_call | solution.py:381

commit v3 on v2

--- a/solution.py
+++ b/solution.py
@@ -76,7 +76,8 @@
         (ops_hbm, ops_ref), (valid_hbm, valid_ref), (trans_hbm, trans_v),
     )):
         loads.append(pltpu.make_async_copy(src, dst, load_sem.at[n]))
-        loads[-1].start()
+    for n in range(3):
+        loads[n].start()
 
     rounds = [[(0, d) for d in spread(ngy)], [(d, 0) for d in spread(ngx)]]
 
@@ -95,6 +96,8 @@
                 pl.semaphore_wait(spread_sem.at[axis, n], 2)
     for n in range(3):
         loads[n].wait()
+    for n in range(3, 7):
+        loads[n].start()
     lane = iota((spheres, LANES), 1)
     eye = iota((cols, cols), 0) == iota((cols, cols), 1)
     kind_col = jnp.concatenate(
@@ -192,8 +195,6 @@
                 ]
 
     loads[6].wait()
-    hear(0)
-    tell(1)
     unit = (iota((LANES, coeffs), 0) == iota((LANES, coeffs), 1)).astype(F32).astype(BF16)
     for k in range(count_ops):
         tt[k, :, :coeffs] = nt(unit, trans_v[k]).astype(BF16)
@@ -202,11 +203,11 @@
         tmlo_t[p, :, :coeffs] = nt(unit, tmlo[p]).astype(BF16)
         mask = jnp.where(jnp.broadcast_to(kind_col, (spheres, LANES)) == p, 1.0, 0.0)
         masks[p] = jnp.concatenate([mask, mask], axis=0).astype(BF16)
-    hear(1)
-    tell(2)
     def couple(h, copies):
         for copy in copies:
             copy.wait_recv()
+        hear(2 * h)
+        tell(2 * h + 1)
         hi, lo = split(mid[h])
         vhi[: 3 * spheres], vlo[: 3 * spheres] = hi, lo
         hi, lo = split(side[h])
@@ -238,8 +239,8 @@
     once = couple(0, flights)
     set_field(1, once)
     flights = exchange(1)
-    hear(2)
-    tell(3)
+    hear(1)
+    tell(2)
     second = couple(1, flights)
     state[2] = second
     base, once = state[0], state[1]
@@ -255,32 +256,70 @@
     packed = jnp.zeros((1, 128), F32)
     for n, value in enumerate(products):
         packed = jnp.where(slot == n, value, packed)
-    def all_sum(n, value, out, into, peers):
-        out[...] = value
-        for d, peer in enumerate(peers):
-            pltpu.make_async_remote_copy(
-                src_ref=out, dst_ref=into.at[d], send_sem=ar_send.at[n], recv_sem=ar_recv.at[n],
-                device_id=peer, device_id_type=MESH,
-            ).start()
-        pltpu.make_async_copy(into, into, ar_recv.at[n]).wait()
-        total = value
-        for d in range(len(peers)):
-            total = total + into[d]
-        return total
+    core = lax.rem(gx, 2)
+    chips, group = ngx // 2, one_in.shape[0]
 
     def far_first(n, inner):
         def hops(d):
             return min(d // inner, n // inner - d // inner) + min(d % inner, inner - d % inner)
 
         return sorted(range(1, n), key=lambda d: -hops(d))
+
+    def along_x(d):
+        return (lax.rem(gx - core + 2 * d + 1, ngx), gy)
+
+    def send(n, out, into, slot, peer):
+        pltpu.make_async_remote_copy(
+            src_ref=out, dst_ref=into.at[slot], send_sem=ar_send.at[n], recv_sem=ar_recv.at[n],
+            device_id=peer, device_id_type=MESH,
+        ).start()
+    one_out[...] = packed
+    for d in far_first(chips, 1):
+
+        @pl.when(core == 1)
+        def _():
+            send(0, one_out, one_in, d - 1, along_x(d))
+
+        @pl.when(core == 0)
+        def _():
+            send(0, one_out, one_in, chips - 1 + d, along_x(d))
+
+    @pl.when(core == 0)
+    def _():
+        send(0, one_out, one_in, chips - 1, along_x(0))
+
     hear(3)
-    packed = all_sum(0, packed, one_out, one_in, [device(0, d) for d in far_first(ngy, 8)])
-    packed = all_sum(1, packed, two_out, two_in, [device(d, 0) for d in far_first(ngx, 2)])
+
+    @pl.when(core == 1)
+    def _():
+        pltpu.make_async_copy(one_in, one_in, ar_recv.at[0]).wait()
+        total = one_out[...]
+        for n in range(group):
+            total = total + one_in[n]
+        two_out[...] = total
+        for c in (-1, 0):
+            for d in far_first(ngy, 8):
+                send(1, two_out, two_in, d, (gx + c, lax.rem(gy + d, ngy)))
+        send(1, two_out, two_in, 0, (gx - 1, gy))
+        two_in[0] = total
+        far = two_in.at[pl.ds(1, ngy - 1)]
+        pltpu.make_async_copy(far, far, ar_recv.at[1]).wait()
+        out = one_in.at[pl.ds(0, chips - 1)]
+        pltpu.make_async_copy(out, out, ar_send.at[0]).wait()
+        pltpu.make_async_copy(two_in, two_in, ar_send.at[1]).wait()
+        pltpu.make_async_copy(far, far, ar_send.at[1]).wait()
+    @pl.when(core == 0)
+    def _():
+        pltpu.make_async_copy(two_in, two_in, ar_recv.at[1]).wait()
+        out = one_in.at[pl.ds(0, chips)]
+        pltpu.make_async_copy(out, out, ar_send.at[0]).wait()
+
+    packed = two_in[0]
+    for n in range(1, ngy):
+        packed = packed + two_in[n]
     sums[...] = packed
     for copy in first_flights + flights:
         copy.wait_send()
-    pltpu.make_async_copy(one_in, one_in, ar_send.at[0]).wait()
-    pltpu.make_async_copy(two_in, two_in, ar_send.at[1]).wait()
 
 
 def combine(state, sums, sol_ref, res_ref):
@@ -365,9 +404,9 @@
                 pltpu.VMEM((3 * spheres + 96, LANES), BF16),
                 pltpu.VMEM((3 * spheres + 96, LANES), BF16),
                 pltpu.VMEM((1, 128), F32),
-                pltpu.VMEM((ngy - 1, 1, 128), F32),
+                pltpu.VMEM((ngx - 1, 1, 128), F32),
                 pltpu.VMEM((1, 128), F32),
-                pltpu.VMEM((ngx - 1, 1, 128), F32),
+                pltpu.VMEM((ngy, 1, 128), F32),
                 pltpu.SemaphoreType.DMA((7,)),
                 pltpu.SemaphoreType.DMA((2, len(PIECES))),
                 pltpu.SemaphoreType.DMA((2, len(PIECES))),

time: 40.4 us -> 42.1 us (1.042)
  Pallas kernels: 39.7 us -> 41.3 us
    pallas_call x1, Pallas kernels: 38.9 us -> 40.5 us  [body(): pl.pallas_call(functools.partial(kernel, ngx, ngy), out_shape=(pltpu.VMEM...]
where the time goes in v3:
time: 42.1 us; the launch traced here: 42 us
  Pallas kernels  41.3 us (98%)
  between operations  0.64 us (2%)
    pallas_call x1, Pallas kernels, body(): pl.pallas_call(functools.partial(kernel, ngx, ngy), out_shape=(pltpu.VMEM...  40.5 us

profile of v3, /device:TPU:1, one launch (start us, length us, event | category | flops | bytes accessed | tf_op | source)
XLA Modules:
  0.0 42.0 jit_solution(14283914846700346095)
XLA Ops:
  0.6 40.5 %shard_map.86 = (f32[3,64,256]{2,1,0:T(8,128)S(1)}, f32[1,128]{1,0:T(1,128)S(1)}) custom-call(f32[4,16,240]{2,1,0:T(8,128)} %inc_hbm.1, s32[4,16]{1,0:T(4,128)} %kinds_hbm.1, s32[4,16,64]{2,1,0:T(8,128)} %codes_hbm.1, s32[4,16,64]{2,1,0:T(8,128)} %ops_hbm.1, s32[4,16,64]{2,1,0:T(8,128)} %valid_hbm.1, bf16[24,240,240]{2,1,0:T(8,128)(2,1)} %trans_hbm.1, ...), custom_call_target="tpu_custom_call" | custom-call | tf_op jit(solution)/shard_map/pallas_call | solution.py:388
  41.1 0.8 %shard_map.87 = (f32[4,16,240]{2,1,0:T(8,128)}, f32[4,16,240]{2,1,0:T(8,128)}) custom-call(f32[3,64,256]{2,1,0:T(8,128)S(1)} %get-tuple-element.4.state, f32[1,128]{1,0:T(1,128)S(1)} %get-tuple-element.5.sums), custom_call_target="tpu_custom_call" | custom-call | tf_op jit(solution)/shard_map/pallas_call | solution.py:420

commit v4 on v2

--- a/solution.py
+++ b/solution.py
@@ -45,7 +45,7 @@
 
 def spread(n):
     steps, d = [], 1
-    while d < n // 2:
+    while d < n - 1:
         steps.append(d)
         d *= 2
     return steps
@@ -67,16 +67,39 @@
 
     def device(dx, dy):
         return (lax.rem(gx + (dx + ngx), ngx), lax.rem(gy + (dy + ngy), ngy))
+
+    def inside_tests(dx, dy):
+        tests = []
+        for at, n, d in ((gx, ngx, dx), (gy, ngy, dy)):
+            if d > 0:
+                tests.append(at < n - d)
+            elif d < 0:
+                tests.append(at >= -d)
+        return tests
+
+    def when(dx, dy):
+        return pl.when(functools.reduce(jnp.logical_and, inside_tests(dx, dy)))
+
+    def count_at(at, size, d):
+        return (at >= d).astype(jnp.int32) + (at < size - d).astype(jnp.int32)
+
+    def there(dx, dy):
+        return (gx + dx, gy + dy)
     barrier = pltpu.get_barrier_semaphore()
     for dx, dy, _, _, _ in PIECES:
-        pl.semaphore_signal(barrier, inc=1, device_id=device(dx, dy), device_id_type=MESH)
+
+        @when(dx, dy)
+        def _():
+            pl.semaphore_signal(barrier, inc=1, device_id=there(dx, dy), device_id_type=MESH)
+
     loads = []
     for n, (src, dst) in enumerate((
         (tmat_hbm, tmat_v), (inc_hbm, inc_ref), (kinds_hbm, kinds_ref), (codes_hbm, codes_ref),
         (ops_hbm, ops_ref), (valid_hbm, valid_ref), (trans_hbm, trans_v),
     )):
         loads.append(pltpu.make_async_copy(src, dst, load_sem.at[n]))
-        loads[-1].start()
+    for n in range(3):
+        loads[n].start()
 
     rounds = [[(0, d) for d in spread(ngy)], [(d, 0) for d in spread(ngx)]]
 
@@ -85,16 +108,23 @@
             if n < len(steps):
                 dx, dy = steps[n]
                 for sign in (1, -1):
-                    pl.semaphore_signal(
-                        spread_sem.at[axis, n], inc=1, device_id=device(sign * dx, sign * dy), device_id_type=MESH
-                    )
+
+                    @when(sign * dx, sign * dy)
+                    def _():
+                        pl.semaphore_signal(
+                            spread_sem.at[axis, n], inc=1, device_id=there(sign * dx, sign * dy), device_id_type=MESH
+                        )
+
 
     def hear(n):
         for axis, steps in enumerate(rounds):
             if n < len(steps):
-                pl.semaphore_wait(spread_sem.at[axis, n], 2)
+                at, size = ((gy, ngy), (gx, ngx))[axis]
+                pl.semaphore_wait(spread_sem.at[axis, n], count_at(at, size, sum(steps[n])))
     for n in range(3):
         loads[n].wait()
+    for n in range(3, 7):
+        loads[n].start()
     lane = iota((spheres, LANES), 1)
     eye = iota((cols, cols), 0) == iota((cols, cols), 1)
     kind_col = jnp.concatenate(
@@ -135,8 +165,7 @@
                     h, spheres + cols * r + c : spheres + cols * r + c + HALO, :
                 ]
 
-    def exchange(h):
-        copies = []
+    def pieces(h):
         for n, (dx, dy, source, first, count) in enumerate(PIECES):
             if source == 0:
                 src, dst = mid.at[h, pl.ds(spheres, spheres)], mid.at[h, pl.ds(first, count)]
@@ -144,11 +173,28 @@
                 src, dst = edge.at[h, source - 1], side.at[h, pl.ds(first, count)]
             copy = pltpu.make_async_remote_copy(
                 src_ref=src, dst_ref=dst, send_sem=halo_send.at[h, n], recv_sem=halo_recv.at[h, n],
-                device_id=device(dx, dy), device_id_type=MESH,
+                device_id=there(dx, dy), device_id_type=MESH,
             )
-            copy.start()
-            copies.append(copy)
-        return copies
+            yield dx, dy, copy
+
+    def exchange(h):
+        for dx, dy, copy in pieces(h):
+            when(dx, dy)(copy.start)
+
+    def arrive(h):
+        for dx, dy, copy in pieces(h):
+            when(-dx, -dy)(copy.wait_recv)
+
+    def sent(h):
+        for dx, dy, copy in pieces(h):
+            when(dx, dy)(copy.wait_send)
+
+    for dx, dy, source, first, count in PIECES:
+
+        @pl.when(jnp.logical_not(functools.reduce(jnp.logical_and, inside_tests(-dx, -dy))))
+        def _():
+            for h in range(2):
+                (mid if source == 0 else side)[h, first : first + count, :] = jnp.zeros((count, LANES), F32)
 
     for p in range(kinds_n):
         hi, lo = split(tmat_v[p])
@@ -157,8 +203,9 @@
     state[0] = jnp.zeros((spheres, LANES), F32)
     state[0, :, :coeffs] = source_of(inc_ref[...].reshape(spheres, coeffs))
     set_field(0, state[0])
-    pl.semaphore_wait(barrier, len(PIECES))
-    flights = exchange(0)
+    near_x, near_y = count_at(gx, ngx, 1), count_at(gy, ngy, 1)
+    pl.semaphore_wait(barrier, (near_x + 1) * (near_y + 1) - 1)
+    exchange(0)
     tell(0)
     for n in range(3, 6):
         loads[n].wait()
@@ -192,8 +239,6 @@
                 ]
 
     loads[6].wait()
-    hear(0)
-    tell(1)
     unit = (iota((LANES, coeffs), 0) == iota((LANES, coeffs), 1)).astype(F32).astype(BF16)
     for k in range(count_ops):
         tt[k, :, :coeffs] = nt(unit, trans_v[k]).astype(BF16)
@@ -202,11 +247,10 @@
         tmlo_t[p, :, :coeffs] = nt(unit, tmlo[p]).astype(BF16)
         mask = jnp.where(jnp.broadcast_to(kind_col, (spheres, LANES)) == p, 1.0, 0.0)
         masks[p] = jnp.concatenate([mask, mask], axis=0).astype(BF16)
-    hear(1)
-    tell(2)
-    def couple(h, copies):
-        for copy in copies:
-            copy.wait_recv()
+    def couple(h):
+        arrive(h)
+        hear(2 * h)
+        tell(2 * h + 1)
         hi, lo = split(mid[h])
         vhi[: 3 * spheres], vlo[: 3 * spheres] = hi, lo
         hi, lo = split(side[h])
@@ -231,16 +275,18 @@
             term = nn(jnp.concatenate([hi, lo], axis=0), tt[k])
             total = term if total is None else total + term
         moved = jnp.where(lane < coeffs, total[:spheres] + total[spheres:], 0.0)
+        if h == 1:
+            hear(3)
+            tell(4)
         result = apply_kinds(moved)
         return result
 
-    first_flights = flights
-    once = couple(0, flights)
+    once = couple(0)
     set_field(1, once)
-    flights = exchange(1)
-    hear(2)
-    tell(3)
-    second = couple(1, flights)
+    exchange(1)
+    hear(1)
+    tell(2)
+    second = couple(1)
     state[2] = second
     base, once = state[0], state[1]
 
@@ -273,12 +319,12 @@
             return min(d // inner, n // inner - d // inner) + min(d % inner, inner - d % inner)
 
         return sorted(range(1, n), key=lambda d: -hops(d))
-    hear(3)
-    packed = all_sum(0, packed, one_out, one_in, [device(0, d) for d in far_first(ngy, 8)])
-    packed = all_sum(1, packed, two_out, two_in, [device(d, 0) for d in far_first(ngx, 2)])
+    packed = all_sum(0, packed, one_out, one_in, [device(d, 0) for d in far_first(ngx, 2)])
+    hear(4)
+    packed = all_sum(1, packed, two_out, two_in, [device(0, d) for d in far_first(ngy, 8)])
     sums[...] = packed
-    for copy in first_flights + flights:
-        copy.wait_send()
+    sent(0)
+    sent(1)
     pltpu.make_async_copy(one_in, one_in, ar_send.at[0]).wait()
     pltpu.make_async_copy(two_in, two_in, ar_send.at[1]).wait()
 
@@ -365,15 +411,15 @@
                 pltpu.VMEM((3 * spheres + 96, LANES), BF16),
                 pltpu.VMEM((3 * spheres + 96, LANES), BF16),
                 pltpu.VMEM((1, 128), F32),
+                pltpu.VMEM((ngx - 1, 1, 128), F32),
+                pltpu.VMEM((1, 128), F32),
                 pltpu.VMEM((ngy - 1, 1, 128), F32),
-                pltpu.VMEM((1, 128), F32),
-                pltpu.VMEM((ngx - 1, 1, 128), F32),
                 pltpu.SemaphoreType.DMA((7,)),
                 pltpu.SemaphoreType.DMA((2, len(PIECES))),
                 pltpu.SemaphoreType.DMA((2, len(PIECES))),
                 pltpu.SemaphoreType.DMA((2,)),
                 pltpu.SemaphoreType.DMA((2,)),
-                pltpu.SemaphoreType.REGULAR((2, 4)),
+                pltpu.SemaphoreType.REGULAR((2, 5)),
             ],
             compiler_params=pltpu.CompilerParams(collective_id=0, has_side_effects=True),
         )(*args)

time: 40.4 us -> 39.8 us (0.985)
  Pallas kernels: 39.7 us -> 39 us
    pallas_call x1, Pallas kernels: 38.9 us -> 38.1 us  [body(): pl.pallas_call(functools.partial(kernel, ngx, ngy), out_shape=(pltpu.VMEM...]
where the time goes in v4:
time: 39.8 us; the launch traced here: 39.6 us
  Pallas kernels  39 us (98%)
  between operations  0.64 us (2%)
    pallas_call x1, Pallas kernels, body(): pl.pallas_call(functools.partial(kernel, ngx, ngy), out_shape=(pltpu.VMEM...  38.1 us
    pallas_call x1, Pallas kernels, body(): pl.pallas_call(combine, out_shape=(jax.ShapeDtypeStruct(incident.shape, F...  0.83 us

profile of v4, /device:TPU:1, one launch (start us, length us, event | category | flops | bytes accessed | tf_op | source)
XLA Modules:
  0.0 39.6 jit_solution(7184476687534035492)
XLA Ops:
  0.6 38.1 %shard_map.86 = (f32[3,64,256]{2,1,0:T(8,128)S(1)}, f32[1,128]{1,0:T(1,128)S(1)}) custom-call(f32[4,16,240]{2,1,0:T(8,128)} %inc_hbm.1, s32[4,16]{1,0:T(4,128)} %kinds_hbm.1, s32[4,16,64]{2,1,0:T(8,128)} %codes_hbm.1, s32[4,16,64]{2,1,0:T(8,128)} %ops_hbm.1, s32[4,16,64]{2,1,0:T(8,128)} %valid_hbm.1, bf16[24,240,240]{2,1,0:T(8,128)(2,1)} %trans_hbm.1, ...), custom_call_target="tpu_custom_call" | custom-call | tf_op jit(solution)/shard_map/pallas_call | solution.py:395
  38.8 0.8 %shard_map.87 = (f32[4,16,240]{2,1,0:T(8,128)}, f32[4,16,240]{2,1,0:T(8,128)}) custom-call(f32[3,64,256]{2,1,0:T(8,128)S(1)} %get-tuple-element.4.state, f32[1,128]{1,0:T(1,128)S(1)} %get-tuple-element.5.sums), custom_call_target="tpu_custom_call" | custom-call | tf_op jit(solution)/shard_map/pallas_call | solution.py:427

commit v5 on v4

--- a/solution.py
+++ b/solution.py
@@ -247,10 +247,13 @@
         tmlo_t[p, :, :coeffs] = nt(unit, tmlo[p]).astype(BF16)
         mask = jnp.where(jnp.broadcast_to(kind_col, (spheres, LANES)) == p, 1.0, 0.0)
         masks[p] = jnp.concatenate([mask, mask], axis=0).astype(BF16)
+    hear(0)
+    tell(1)
     def couple(h):
         arrive(h)
-        hear(2 * h)
-        tell(2 * h + 1)
+        if h == 0:
+            hear(1)
+            tell(2)
         hi, lo = split(mid[h])
         vhi[: 3 * spheres], vlo[: 3 * spheres] = hi, lo
         hi, lo = split(side[h])
@@ -275,17 +278,14 @@
             term = nn(jnp.concatenate([hi, lo], axis=0), tt[k])
             total = term if total is None else total + term
         moved = jnp.where(lane < coeffs, total[:spheres] + total[spheres:], 0.0)
-        if h == 1:
-            hear(3)
-            tell(4)
         result = apply_kinds(moved)
         return result
 
     once = couple(0)
     set_field(1, once)
     exchange(1)
-    hear(1)
-    tell(2)
+    hear(2)
+    tell(3)
     second = couple(1)
     state[2] = second
     base, once = state[0], state[1]
@@ -319,6 +319,8 @@
             return min(d // inner, n // inner - d // inner) + min(d % inner, inner - d % inner)
 
         return sorted(range(1, n), key=lambda d: -hops(d))
+    hear(3)
+    tell(4)
     packed = all_sum(0, packed, one_out, one_in, [device(d, 0) for d in far_first(ngx, 2)])
     hear(4)
     packed = all_sum(1, packed, two_out, two_in, [device(0, d) for d in far_first(ngy, 8)])

time: 39.8 us -> 39.6 us (level)
  no operation moved by 1% of the time
where the time goes in v5:
time: 39.6 us; the launch traced here: 39.5 us
  Pallas kernels  38.9 us (98%)
  between operations  0.64 us (2%)
    pallas_call x1, Pallas kernels, body(): pl.pallas_call(functools.partial(kernel, ngx, ngy), out_shape=(pltpu.VMEM...  38 us
    pallas_call x1, Pallas kernels, body(): pl.pallas_call(combine, out_shape=(jax.ShapeDtypeStruct(incident.shape, F...  0.83 us

profile of v5, /device:TPU:1, one launch (start us, length us, event | category | flops | bytes accessed | tf_op | source)
XLA Modules:
  0.0 39.5 jit_solution(1726824555363128111)
XLA Ops:
  0.6 38.0 %shard_map.86 = (f32[3,64,256]{2,1,0:T(8,128)S(1)}, f32[1,128]{1,0:T(1,128)S(1)}) custom-call(f32[4,16,240]{2,1,0:T(8,128)} %inc_hbm.1, s32[4,16]{1,0:T(4,128)} %kinds_hbm.1, s32[4,16,64]{2,1,0:T(8,128)} %codes_hbm.1, s32[4,16,64]{2,1,0:T(8,128)} %ops_hbm.1, s32[4,16,64]{2,1,0:T(8,128)} %valid_hbm.1, bf16[24,240,240]{2,1,0:T(8,128)(2,1)} %trans_hbm.1, ...), custom_call_target="tpu_custom_call" | custom-call | tf_op jit(solution)/shard_map/pallas_call | solution.py:397
  38.7 0.8 %shard_map.87 = (f32[4,16,240]{2,1,0:T(8,128)}, f32[4,16,240]{2,1,0:T(8,128)}) custom-call(f32[3,64,256]{2,1,0:T(8,128)S(1)} %get-tuple-element.4.state, f32[1,128]{1,0:T(1,128)S(1)} %get-tuple-element.5.sums), custom_call_target="tpu_custom_call" | custom-call | tf_op jit(solution)/shard_map/pallas_call | solution.py:429

commit v6 on v5

--- a/solution.py
+++ b/solution.py
@@ -239,6 +239,8 @@
                 ]
 
     loads[6].wait()
+    hear(0)
+    tell(1)
     unit = (iota((LANES, coeffs), 0) == iota((LANES, coeffs), 1)).astype(F32).astype(BF16)
     for k in range(count_ops):
         tt[k, :, :coeffs] = nt(unit, trans_v[k]).astype(BF16)
@@ -247,8 +249,6 @@
         tmlo_t[p, :, :coeffs] = nt(unit, tmlo[p]).astype(BF16)
         mask = jnp.where(jnp.broadcast_to(kind_col, (spheres, LANES)) == p, 1.0, 0.0)
         masks[p] = jnp.concatenate([mask, mask], axis=0).astype(BF16)
-    hear(0)
-    tell(1)
     def couple(h):
         arrive(h)
         if h == 0:

time: 39.6 us -> 38.7 us (0.977)
  Pallas kernels: 38.9 us -> 37.9 us
    pallas_call x1, Pallas kernels: 38 us -> 37.1 us  [body(): pl.pallas_call(functools.partial(kernel, ngx, ngy), out_shape=(pltpu.VMEM...]
where the time goes in v6:
time: 38.7 us; the launch traced here: 38.5 us
  Pallas kernels  37.9 us (98%)
  between operations  0.64 us (2%)
    pallas_call x1, Pallas kernels, body(): pl.pallas_call(functools.partial(kernel, ngx, ngy), out_shape=(pltpu.VMEM...  37.1 us
    pallas_call x1, Pallas kernels, body(): pl.pallas_call(combine, out_shape=(jax.ShapeDtypeStruct(incident.shape, F...  0.83 us

profile of v6, /device:TPU:1, one launch (start us, length us, event | category | flops | bytes accessed | tf_op | source)
XLA Modules:
  0.0 38.5 jit_solution(8785294438614714236)
XLA Ops:
  0.6 37.1 %shard_map.86 = (f32[3,64,256]{2,1,0:T(8,128)S(1)}, f32[1,128]{1,0:T(1,128)S(1)}) custom-call(f32[4,16,240]{2,1,0:T(8,128)} %inc_hbm.1, s32[4,16]{1,0:T(4,128)} %kinds_hbm.1, s32[4,16,64]{2,1,0:T(8,128)} %codes_hbm.1, s32[4,16,64]{2,1,0:T(8,128)} %ops_hbm.1, s32[4,16,64]{2,1,0:T(8,128)} %valid_hbm.1, bf16[24,240,240]{2,1,0:T(8,128)(2,1)} %trans_hbm.1, ...), custom_call_target="tpu_custom_call" | custom-call | tf_op jit(solution)/shard_map/pallas_call | solution.py:397
  37.7 0.8 %shard_map.87 = (f32[4,16,240]{2,1,0:T(8,128)}, f32[4,16,240]{2,1,0:T(8,128)}) custom-call(f32[3,64,256]{2,1,0:T(8,128)S(1)} %get-tuple-element.4.state, f32[1,128]{1,0:T(1,128)S(1)} %get-tuple-element.5.sums), custom_call_target="tpu_custom_call" | custom-call | tf_op jit(solution)/shard_map/pallas_call | solution.py:429

commit v7 on v6

--- a/solution.py
+++ b/solution.py
@@ -54,7 +54,7 @@
 def kernel(
     ngx, ngy, inc_hbm, kinds_hbm, codes_hbm, ops_hbm, valid_hbm, trans_hbm, tmat_hbm,
     state, sums,
-    inc_ref, kinds_ref, codes_ref, ops_ref, valid_ref, trans_v, tmat_v,
+    inc_ref, kinds_ref, pairs, trans_v, tmat_v,
     tmhi, tmlo, tmhi_t, tmlo_t, masks, tt, counts, grouped, mid, side, edge, vhi, vlo,
     one_out, one_in, two_out, two_in,
     load_sem, halo_send, halo_recv, ar_send, ar_recv, spread_sem,
@@ -62,7 +62,7 @@
     gx, gy = lax.axis_index("gx"), lax.axis_index("gy")
     rows, cols, coeffs = inc_ref.shape
     spheres = rows * cols
-    slots = codes_ref.shape[2]
+    slots = pairs.shape[3]
     count_ops, kinds_n = trans_v.shape[0], tmat_v.shape[0]
 
     def device(dx, dy):
@@ -92,14 +92,12 @@
         def _():
             pl.semaphore_signal(barrier, inc=1, device_id=there(dx, dy), device_id_type=MESH)
 
-    loads = []
-    for n, (src, dst) in enumerate((
-        (tmat_hbm, tmat_v), (inc_hbm, inc_ref), (kinds_hbm, kinds_ref), (codes_hbm, codes_ref),
-        (ops_hbm, ops_ref), (valid_hbm, valid_ref), (trans_hbm, trans_v),
-    )):
-        loads.append(pltpu.make_async_copy(src, dst, load_sem.at[n]))
-    for n in range(3):
-        loads[n].start()
+    def load(src, dst, n):
+        copy = pltpu.make_async_copy(src, dst, load_sem.at[n])
+        copy.start()
+        return copy
+
+    early = [load(tmat_hbm, tmat_v, 0), load(inc_hbm, inc_ref, 1), load(kinds_hbm, kinds_ref, 2)]
 
     rounds = [[(0, d) for d in spread(ngy)], [(d, 0) for d in spread(ngx)]]
 
@@ -112,19 +110,22 @@
                     @when(sign * dx, sign * dy)
                     def _():
                         pl.semaphore_signal(
-                            spread_sem.at[axis, n], inc=1, device_id=there(sign * dx, sign * dy), device_id_type=MESH
+                            spread_sem.at[n], inc=1, device_id=there(sign * dx, sign * dy), device_id_type=MESH
                         )
 
 
     def hear(n):
-        for axis, steps in enumerate(rounds):
+        expected = 0
+        for (at, size), steps in zip(((gy, ngy), (gx, ngx)), rounds):
             if n < len(steps):
-                at, size = ((gy, ngy), (gx, ngx))[axis]
-                pl.semaphore_wait(spread_sem.at[axis, n], count_at(at, size, sum(steps[n])))
-    for n in range(3):
-        loads[n].wait()
-    for n in range(3, 7):
-        loads[n].start()
+                expected = expected + count_at(at, size, sum(steps[n]))
+        if n < max(map(len, rounds)):
+            pl.semaphore_wait(spread_sem.at[n], expected)
+    for copy in early:
+        copy.wait()
+    for n, src in enumerate((codes_hbm, ops_hbm, valid_hbm)):
+        load(src, pairs.at[n], 0)
+    late = load(trans_hbm, trans_v, 1)
     lane = iota((spheres, LANES), 1)
     eye = iota((cols, cols), 0) == iota((cols, cols), 1)
     kind_col = jnp.concatenate(
@@ -172,7 +173,7 @@
             else:
                 src, dst = edge.at[h, source - 1], side.at[h, pl.ds(first, count)]
             copy = pltpu.make_async_remote_copy(
-                src_ref=src, dst_ref=dst, send_sem=halo_send.at[h, n], recv_sem=halo_recv.at[h, n],
+                src_ref=src, dst_ref=dst, send_sem=halo_send.at[h], recv_sem=halo_recv.at[h],
                 device_id=there(dx, dy), device_id_type=MESH,
             )
             yield dx, dy, copy
@@ -181,13 +182,16 @@
         for dx, dy, copy in pieces(h):
             when(dx, dy)(copy.start)
 
-    def arrive(h):
-        for dx, dy, copy in pieces(h):
-            when(-dx, -dy)(copy.wait_recv)
-
-    def sent(h):
-        for dx, dy, copy in pieces(h):
-            when(dx, dy)(copy.wait_send)
+    def all_pieces(sem):
+        for x in (1, 2):
+            for y in (1, 2):
+
+                @pl.when(jnp.logical_and(near_x == x, near_y == y))
+                def _():
+                    much = counts.at[0, pl.ds(0, 2 * (spheres * x + 16 * y * (x + 1)))]
+                    pltpu.make_async_copy(much, much, sem).wait()
+
+    near_x, near_y = count_at(gx, ngx, 1), count_at(gy, ngy, 1)
 
     for dx, dy, source, first, count in PIECES:
 
@@ -203,13 +207,11 @@
     state[0] = jnp.zeros((spheres, LANES), F32)
     state[0, :, :coeffs] = source_of(inc_ref[...].reshape(spheres, coeffs))
     set_field(0, state[0])
-    near_x, near_y = count_at(gx, ngx, 1), count_at(gy, ngy, 1)
     pl.semaphore_wait(barrier, (near_x + 1) * (near_y + 1) - 1)
     exchange(0)
     tell(0)
-    for n in range(3, 6):
-        loads[n].wait()
-    codes = codes_ref[...].reshape(spheres, slots)
+    pltpu.make_async_copy(pairs, pairs, load_sem.at[0]).wait()
+    codes = pairs[0].reshape(spheres, slots)
     sphere = iota((spheres, slots), 0)
     row, col = sphere >> 4, sphere & 15
     step_x = (codes * 57) >> 9
@@ -223,8 +225,8 @@
     at_x = gx * rows + ext_x - HALO
     at_y = gy * cols + ext_y - HALO
     inside = (at_x >= 0) & (at_x < ngx * rows) & (at_y >= 0) & (at_y < ngy * cols)
-    inside = inside & (valid_ref[...].reshape(spheres, slots) == 1)
-    key = jnp.where(inside, row * count_ops + ops_ref[...].reshape(spheres, slots), -1)
+    inside = inside & (pairs[2].reshape(spheres, slots) == 1)
+    key = jnp.where(inside, row * count_ops + pairs[1].reshape(spheres, slots), -1)
     target = jnp.concatenate([target[cols * r : cols * (r + 1)] for r in range(rows)], axis=1)
     key = jnp.concatenate([key[cols * r : cols * (r + 1)] for r in range(rows)], axis=1)
     for c in range(cols):
@@ -238,7 +240,7 @@
                     :, 128 * half : 128 * (half + 1)
                 ]
 
-    loads[6].wait()
+    late.wait()
     hear(0)
     tell(1)
     unit = (iota((LANES, coeffs), 0) == iota((LANES, coeffs), 1)).astype(F32).astype(BF16)
@@ -250,7 +252,7 @@
         mask = jnp.where(jnp.broadcast_to(kind_col, (spheres, LANES)) == p, 1.0, 0.0)
         masks[p] = jnp.concatenate([mask, mask], axis=0).astype(BF16)
     def couple(h):
-        arrive(h)
+        all_pieces(halo_recv.at[h])
         if h == 0:
             hear(1)
             tell(2)
@@ -305,10 +307,11 @@
         out[...] = value
         for d, peer in enumerate(peers):
             pltpu.make_async_remote_copy(
-                src_ref=out, dst_ref=into.at[d], send_sem=ar_send.at[n], recv_sem=ar_recv.at[n],
+                src_ref=out, dst_ref=into.at[d], send_sem=ar_send, recv_sem=ar_recv.at[n],
                 device_id=peer, device_id_type=MESH,
             ).start()
         pltpu.make_async_copy(into, into, ar_recv.at[n]).wait()
+        pltpu.make_async_copy(into, into, ar_send).wait()
         total = value
         for d in range(len(peers)):
             total = total + into[d]
@@ -325,10 +328,8 @@
     hear(4)
     packed = all_sum(1, packed, two_out, two_in, [device(0, d) for d in far_first(ngy, 8)])
     sums[...] = packed
-    sent(0)
-    sent(1)
-    pltpu.make_async_copy(one_in, one_in, ar_send.at[0]).wait()
-    pltpu.make_async_copy(two_in, two_in, ar_send.at[1]).wait()
+    all_pieces(halo_send.at[0])
+    all_pieces(halo_send.at[1])
 
 
 def combine(state, sums, sol_ref, res_ref):
@@ -394,12 +395,14 @@
         vmem = pl.BlockSpec(memory_space=pltpu.VMEM)
         hbm = pl.BlockSpec(memory_space=pltpu.HBM)
         args = (incident, sphere_kinds, pair_codes, operators, pair_valid, translations, tmatrices)
+        held = [(arg.shape, arg.dtype) for arg in args]
+        held[2:5] = [((3, *pair_codes.shape), jnp.int32)]
         state, sums = pl.pallas_call(
             functools.partial(kernel, ngx, ngy),
             out_shape=(pltpu.VMEM((3, spheres, LANES), F32), pltpu.VMEM((1, 128), F32)),
             in_specs=[hbm] * 7,
             out_specs=(vmem, vmem),
-            scratch_shapes=[pltpu.VMEM(arg.shape, arg.dtype) for arg in args]
+            scratch_shapes=[pltpu.VMEM(shape, kind) for shape, kind in held]
             + [pltpu.VMEM(tmatrices.shape, BF16)] * 2
             + [pltpu.VMEM((kinds_n, LANES, LANES), BF16)] * 2
             + [
@@ -416,12 +419,12 @@
                 pltpu.VMEM((ngx - 1, 1, 128), F32),
                 pltpu.VMEM((1, 128), F32),
                 pltpu.VMEM((ngy - 1, 1, 128), F32),
-                pltpu.SemaphoreType.DMA((7,)),
-                pltpu.SemaphoreType.DMA((2, len(PIECES))),
-                pltpu.SemaphoreType.DMA((2, len(PIECES))),
+                pltpu.SemaphoreType.DMA((3,)),
                 pltpu.SemaphoreType.DMA((2,)),
                 pltpu.SemaphoreType.DMA((2,)),
-                pltpu.SemaphoreType.REGULAR((2, 5)),
+                pltpu.SemaphoreType.DMA,
+                pltpu.SemaphoreType.DMA((2,)),
+                pltpu.SemaphoreType.REGULAR((5,)),
             ],
             compiler_params=pltpu.CompilerParams(collective_id=0, has_side_effects=True),
         )(*args)

time: 38.7 us -> 38.3 us (0.990)
  Pallas kernels: 37.9 us -> 37.5 us
where the time goes in v7:
time: 38.3 us; the launch traced here: 38.1 us
  Pallas kernels  37.5 us (98%)
  between operations  0.64 us (2%)
    pallas_call x1, Pallas kernels, body(): pl.pallas_call(functools.partial(kernel, ngx, ngy), out_shape=(pltpu.VMEM...  36.7 us
    pallas_call x1, Pallas kernels, body(): pl.pallas_call(combine, out_shape=(jax.ShapeDtypeStruct(incident.shape, F...  0.83 us

profile of v7, /device:TPU:1, one launch (start us, length us, event | category | flops | bytes accessed | tf_op | source)
XLA Modules:
  0.0 38.1 jit_solution(18184147803236682020)
XLA Ops:
  0.6 36.7 %shard_map.86 = (f32[3,64,256]{2,1,0:T(8,128)S(1)}, f32[1,128]{1,0:T(1,128)S(1)}) custom-call(f32[4,16,240]{2,1,0:T(8,128)} %inc_hbm.1, s32[4,16]{1,0:T(4,128)} %kinds_hbm.1, s32[4,16,64]{2,1,0:T(8,128)} %codes_hbm.1, s32[4,16,64]{2,1,0:T(8,128)} %ops_hbm.1, s32[4,16,64]{2,1,0:T(8,128)} %valid_hbm.1, bf16[24,240,240]{2,1,0:T(8,128)(2,1)} %trans_hbm.1, ...), custom_call_target="tpu_custom_call" | custom-call | tf_op jit(solution)/shard_map/pallas_call | solution.py:400
  37.3 0.8 %shard_map.87 = (f32[4,16,240]{2,1,0:T(8,128)}, f32[4,16,240]{2,1,0:T(8,128)}) custom-call(f32[3,64,256]{2,1,0:T(8,128)S(1)} %get-tuple-element.4.state, f32[1,128]{1,0:T(1,128)S(1)} %get-tuple-element.5.sums), custom_call_target="tpu_custom_call" | custom-call | tf_op jit(solution)/shard_map/pallas_call | solution.py:432

commit v8 on v7

--- a/solution.py
+++ b/solution.py
@@ -253,9 +253,6 @@
         masks[p] = jnp.concatenate([mask, mask], axis=0).astype(BF16)
     def couple(h):
         all_pieces(halo_recv.at[h])
-        if h == 0:
-            hear(1)
-            tell(2)
         hi, lo = split(mid[h])
         vhi[: 3 * spheres], vlo[: 3 * spheres] = hi, lo
         hi, lo = split(side[h])
@@ -280,6 +277,9 @@
             term = nn(jnp.concatenate([hi, lo], axis=0), tt[k])
             total = term if total is None else total + term
         moved = jnp.where(lane < coeffs, total[:spheres] + total[spheres:], 0.0)
+        if h == 0:
+            hear(1)
+            tell(2)
         result = apply_kinds(moved)
         return result
 

time: 38.3 us -> 38.4 us (level)
  no operation moved by 1% of the time
where the time goes in v8:
time: 38.4 us; the launch traced here: 38.2 us
  Pallas kernels  37.6 us (98%)
  between operations  0.64 us (2%)
    pallas_call x1, Pallas kernels, body(): pl.pallas_call(functools.partial(kernel, ngx, ngy), out_shape=(pltpu.VMEM...  36.7 us
    pallas_call x1, Pallas kernels, body(): pl.pallas_call(combine, out_shape=(jax.ShapeDtypeStruct(incident.shape, F...  0.83 us

profile of v8, /device:TPU:1, one launch (start us, length us, event | category | flops | bytes accessed | tf_op | source)
XLA Modules:
  0.0 38.2 jit_solution(2996210431773479479)
XLA Ops:
  0.6 36.7 %shard_map.86 = (f32[3,64,256]{2,1,0:T(8,128)S(1)}, f32[1,128]{1,0:T(1,128)S(1)}) custom-call(f32[4,16,240]{2,1,0:T(8,128)} %inc_hbm.1, s32[4,16]{1,0:T(4,128)} %kinds_hbm.1, s32[4,16,64]{2,1,0:T(8,128)} %codes_hbm.1, s32[4,16,64]{2,1,0:T(8,128)} %ops_hbm.1, s32[4,16,64]{2,1,0:T(8,128)} %valid_hbm.1, bf16[24,240,240]{2,1,0:T(8,128)(2,1)} %trans_hbm.1, ...), custom_call_target="tpu_custom_call" | custom-call | tf_op jit(solution)/shard_map/pallas_call | solution.py:400
  37.4 0.8 %shard_map.87 = (f32[4,16,240]{2,1,0:T(8,128)}, f32[4,16,240]{2,1,0:T(8,128)}) custom-call(f32[3,64,256]{2,1,0:T(8,128)S(1)} %get-tuple-element.4.state, f32[1,128]{1,0:T(1,128)S(1)} %get-tuple-element.5.sums), custom_call_target="tpu_custom_call" | custom-call | tf_op jit(solution)/shard_map/pallas_call | solution.py:432
